TPU v7x, 16 devices: a whole 2x2x2 slice. The times are simulated.
16 devices in a mesh: dp: 2 (over z), stage: 2 (over y), tp: 4 (over x, core).
Axes of the slice: x: 2, y: 2, z: 2, core: 2. Of those that a mesh axis runs over, the one named last changes fastest.
Arguments:
- act_in: bfloat16 [2, 24, 14, 14, 1024], P('stage', ('dp', 'tp'))
- w_conv: bfloat16 [2, 3, 3, 1024, 1024], P('stage', None, None, 'tp')
- w_short: bfloat16 [2, 1024, 1024], P('stage', 'tp')
- gamma: float32 [2, 1024], P('stage', 'tp')
- beta: float32 [2, 1024], P('stage', 'tp')
- gamma_s: float32 [2, 1024], P('stage', 'tp')
- grad_z: bfloat16 [2, 24, 14, 14, 1024], P('stage', 'dp', None, None, 'tp')
Outputs:
- output 1: bfloat16 [2, 24, 14, 14, 1024], P('stage', 'dp', None, None, 'tp')
- output 2: bfloat16 [2, 24, 14, 14, 1024], P('stage', ('dp', 'tp'))
- output 3: float32 [2, 3, 3, 1024, 1024], P('stage', None, None, 'tp')
- output 4: float32 [2, 1024, 1024], P('stage', 'tp')
All inputs are finite; a program needn't handle non-finite values.
Results may differ from a plain program's by a relative error of at most 0.00668.
Values are sent between devices in bfloat16 or wider.
A program may use at most 1 GiB of HBM per device.

v0:
```python
import jax
import jax.numpy as jnp
from jax import lax
from jax.sharding import PartitionSpec as P


def conv_same(left_op, right_op, right_spec):
    return lax.conv_general_dilated(left_op, right_op, (1, 1), "SAME", dimension_numbers=("NHWC", right_spec, "NHWC"), preferred_element_type=jnp.float32)


def weight_grad(images_in, grads_out):
    return lax.conv_general_dilated(images_in, grads_out, (1, 1), ((1, 1), (1, 1)), dimension_numbers=("CHWN", "IHWO", "HWNC"), preferred_element_type=jnp.float32)


def solution(mesh):
    act_spec = P("stage", ("dp", "tp"), None, None, None)
    kernel_spec = P("stage", None, None, "tp", None)
    short_spec = P("stage", "tp", None)
    vec_spec = P("stage", "tp")
    grad_spec = P("stage", "dp", None, None, "tp")

    def device_step(act_in, w_conv, w_short, gamma, beta, gamma_s, grad_z):
        by_channel = lax.all_to_all(act_in[0], "tp", 3, 0, tiled=True)
        act_local = lax.ppermute(by_channel, "stage", perm=[(0, 1)])
        kernel = w_conv[0]
        short_w = w_short[0]
        scale_main = gamma[0]
        shift_main = beta[0]
        scale_short = gamma_s[0]
        pre_part = conv_same(act_local, kernel, "HWIO")
        short_part = jnp.einsum("nhwc,co->nhwo", act_local, short_w, preferred_element_type=jnp.float32)
        pre_sum, short_sum = lax.psum_scatter((pre_part, short_part), "tp", scatter_dimension=3, tiled=True)
        mixed_sum = pre_sum * scale_main + shift_main + short_sum * scale_short
        z_val = jnp.maximum(mixed_sum, 0.0).astype(jnp.bfloat16)
        mask_pos = mixed_sum > 0.0
        grad_here = grad_z[0]
        g_main = jnp.where(mask_pos, grad_here * scale_main, 0.0).astype(jnp.bfloat16)
        g_short = jnp.where(mask_pos, grad_here * scale_short, 0.0).astype(jnp.bfloat16)
        g_main_all, g_short_all = lax.all_gather((g_main, g_short), "tp", axis=3, tiled=True)
        grad_wide = conv_same(g_main_all, kernel[::-1, ::-1], "HWOI") + jnp.einsum("nhwo,co->nhwc", g_short_all, short_w, preferred_element_type=jnp.float32)
        grad_local = grad_wide.astype(jnp.bfloat16)
        dw_part = weight_grad(act_local, g_main_all)
        dws_part = jnp.einsum("nhwc,nhwo->co", act_local, g_short_all, preferred_element_type=jnp.float32)
        dw_sum, dws_sum = lax.psum((dw_part, dws_part), "dp")
        returned = lax.ppermute(grad_local, "stage", perm=[(1, 0)])
        grad_act = lax.all_to_all(returned, "tp", 0, 3, tiled=True)
        return z_val[None], grad_act[None], dw_sum[None], dws_sum[None]

    return jax.shard_map(device_step, mesh=mesh, in_specs=(act_spec, kernel_spec, short_spec, vec_spec, vec_spec, vec_spec, grad_spec), out_specs=(grad_spec, act_spec, kernel_spec, short_spec), check_vma=False)
```

profile of v0, /device:TPU:5, one launch (start us, length us, event | category | flops | bytes accessed | tf_op | source)
XLA Modules:
  0.0 710.2 jit_solution(3975340262819298471)
XLA Ops:
  7.2 0.0 copy-start
  7.2 0.0 reduce-scatter.5.cloned.1.call-start
  7.2 14.0 %copy.42 = bf16[1,3,14,14,1024]{3,2,1,4,0:T(8,128)(2,1)} copy(bf16[1,3,14,14,1024]{4,3,2,1,0:T(8,128)(2,1)} %param.7) | data formatting | bytes 2408448 | tf_op args[0]
  21.2 11.3 %bitcast_bitcast_fusion = bf16[1024,3,14,14]{3,2,1,0:T(8,128)(2,1)} fusion(bf16[1,3,14,14,1024]{3,2,1,4,0:T(8,128)(2,1)} %copy.42), kind=kLoop, calls=%fused_computation.26 | loop fusion | bytes 2408448
  32.5 15.1 %reshape.17 = bf16[4,2,75264]{2,1,0:T(2,128)(2,1)S(1)} reshape(bf16[1024,3,14,14]{3,2,1,0:T(8,128)(2,1)} %bitcast_bitcast_fusion) | data formatting | bytes 2408448
  47.6 18.8 %all_to_all.33 = bf16[4,2,75264]{2,1,0:T(2,128)(2,1)S(1)} all-to-all(bf16[4,2,75264]{2,1,0:T(2,128)(2,1)S(1)} %reshape.17), channel_id=1, replica_groups=mesh['dp'=2,'stage'=2,'tp'=4] {'tp'}, dimensions={0} | all-to-all | bytes 2408448 | tf_op jit(solution)/shard_map/all_to_all | solution.py:23
  66.4 15.9 %reshape.18 = bf16[1024,3,14,14]{3,2,1,0:T(8,128)(2,1)} reshape(bf16[4,2,75264]{2,1,0:T(2,128)(2,1)S(1)} %all_to_all.33) | data formatting | bytes 2408448
  82.3 14.8 %copy.57 = bf16[3,14,14,4,256]{4,3,2,1,0:T(4,128)(2,1)S(1)} copy(bf16[3,14,14,4,256]{2,1,0,4,3:T(8,128)(2,1)} %bitcast.50) | data formatting | bytes 2408448 | tf_op jit(solution)/shard_map/all_to_all | solution.py:23
  97.1 0.2 copy.44
  97.4 1.3 collective-permute-start
  98.7 31.8 %collective-permute-done = bf16[12,14,14,256]{3,2,1,0:T(8,128)(2,1)S(1)} collective-permute-done((bf16[12,14,14,256]{3,2,1,0:T(8,128)(2,1)S(1)}, bf16[12,14,14,256]{3,2,1,0:T(8,128)(2,1)S(1)}, u32[]{:S(2)}, u32[]{:S(2)}) %collective-permute-start) | collective-permute-done | bytes 1204256 | tf_op jit(solution)/shard_map/ppermute | solution.py:24
  130.5 0.0 copy-done
  130.5 6.5 fusion.14
  137.0 0.0 reduce-scatter.5.cloned.1.call-update
  137.0 0.2 reduce-scatter.3.cloned.1.call-start
  137.2 19.1 %fusion.2 = f32[12,14,14,1024]{3,0,2,1:T(8,128)} fusion(bf16[1,3,3,256,1024]{4,3,2,1,0:T(8,128)(2,1)} %param.8, bf16[12,14,14,256]{3,2,1,0:T(8,128)(2,1)S(1)} %collective-permute-done), kind=kOutput, calls=%fused_computation.2 | convolution fusion | flops 10066329600 | bytes 15556608 | tf_op jit(solution)/shard_map/conv_general_dilated | solution.py:8
  156.3 0.0 copy-start.2
  156.3 0.0 copy-start.3
  156.3 0.0 copy-start.4
  156.4 0.0 reduce-scatter.3.cloned.1.call-update
  156.4 0.0 all-gather.5.cloned.1.call-start
  156.4 75.2 %reduce-scatter.5.cloned.1.call-done = f32[12,14,14,256]{3,0,2,1:T(8,128)} async-done(((f32[12,14,14,1024]{3,0,2,1:T(8,128)}), f32[12,14,14,256]{3,0,2,1:T(8,128)}) %reduce-scatter.5.cloned.1.call-update) | async-done | bytes 2408464 | tf_op jit(solution)/shard_map/reduce_scatter | solution.py:32
  231.6 96.6 %reduce-scatter.3.cloned.1.call-done = f32[12,14,14,256]{3,0,2,1:T(8,128)} async-done(((f32[12,14,14,1024]{3,0,2,1:T(8,128)}), f32[12,14,14,256]{3,0,2,1:T(8,128)}) %reduce-scatter.3.cloned.1.call-update) | async-done | bytes 2408464 | tf_op jit(solution)/shard_map/reduce_scatter | solution.py:32
  328.2 0.0 copy-done.2
  328.2 0.0 copy-done.3
  328.2 0.0 copy-done.4
  328.2 0.0 copy-start.1
  328.2 6.2 fusion.5
  334.5 0.0 copy-done.1
  334.5 2.5 fusion.7
  336.9 0.0 all-gather.5.cloned.1.call-update
  337.0 0.0 all-gather.3.cloned.1.call-start
  337.0 0.5 all-gather.3.cloned.1.call-update
  337.6 0.3 all-reduce.3.cloned.1.call-start
  337.8 46.1 %all-gather.5.cloned.1.call-done = bf16[12,14,14,1024]{3,0,2,1:T(8,128)(2,1)} async-done(((bf16[12,14,14,256]{3,0,2,1:T(8,128)(2,1)}), bf16[12,14,14,1024]{3,0,2,1:T(8,128)(2,1)}) %all-gather.5.cloned.1.call-update) | async-done | bytes 4816912 | tf_op jit(solution)/shard_map/all_gather | solution.py:39
  383.9 5.9 fusion.17
  389.9 42.2 %all-gather.3.cloned.1.call-done = bf16[12,14,14,1024]{3,0,2,1:T(8,128)(2,1)} async-done(((bf16[12,14,14,256]{3,0,2,1:T(8,128)(2,1)}), bf16[12,14,14,1024]{3,0,2,1:T(8,128)(2,1)}) %all-gather.3.cloned.1.call-update) | async-done | bytes 4816912 | tf_op jit(solution)/shard_map/all_gather | solution.py:39
  432.1 20.6 %convolution_bitcast_fusion = f32[1,3,3,256,1024]{4,3,2,1,0:T(8,128)} fusion(bf16[12,14,14,1024]{3,0,2,1:T(8,128)(2,1)} %all-gather.3.cloned.1.call-done, bf16[12,14,14,256]{3,2,1,0:T(8,128)(2,1)S(1)} %collective-permute-done), kind=kOutput, calls=%fused_computation.6 | convolution fusion | flops 10066329600 | bytes 15458304 | tf_op jit(solution)/shard_map/conv_general_dilated | solution.py:12
  452.6 0.0 all-reduce.3.cloned.1.call-update
  452.6 4.7 fusion.20
  457.3 20.0 %add_convert_fusion = bf16[12,14,14,256]{3,0,2,1:T(8,128)(2,1)S(1)} fusion(f32[12,14,14,256]{3,0,2,1:T(8,128)S(1)} %fusion.20, bf16[12,14,14,1024]{3,0,2,1:T(8,128)(2,1)} %all-gather.3.cloned.1.call-done, bf16[1,3,3,256,1024]{4,3,2,1,0:T(8,128)(2,1)} %param.8), kind=kOutput, calls=%fused_computation.11 | convolution fusion | flops 10067533824 | bytes 13148160 | tf_op jit(solution)/shard_map/conv_general_dilated | solution.py:8
  477.4 0.4 copy.48
  477.8 3.3 collective-permute-start.1
  481.1 28.1 %collective-permute-done.1 = bf16[12,14,14,256]{3,2,1,0:T(8,128)(2,1)} collective-permute-done((bf16[12,14,14,256]{3,2,1,0:T(8,128)(2,1)S(1)}, bf16[12,14,14,256]{3,2,1,0:T(8,128)(2,1)}, u32[]{:S(2)}, u32[]{:S(2)}) %collective-permute-start.1) | collective-permute-done | bytes 1204256 | tf_op jit(solution)/shard_map/ppermute | solution.py:45
  509.2 4.6 all-to-all-start.1
  513.9 1.5 copy.52
  515.4 15.4 %all-to-all-done.1 = bf16[12,14,14,256]{3,2,1,0:T(8,128)(2,1)S(1)} async-done(((bf16[12,14,14,256]{3,2,1,0:T(8,128)(2,1)}), bf16[12,14,14,256]{3,2,1,0:T(8,128)(2,1)S(1)}, u32[]{:S(2)}, u32[]{:S(2)}) %all-to-all-start.1) | async-done | bytes 1204256 | tf_op jit(solution)/shard_map/all_to_all | solution.py:46
  530.7 0.9 copy.49
  531.7 1.6 broadcast_in_dim.16
  533.3 158.0 %all-reduce.3.cloned.1.call-done = (f32[1,3,3,256,1024]{4,3,2,1,0:T(8,128)}, f32[1,256,1024]{1,2,0:T(8,128)}) async-done(((f32[1,3,3,256,1024]{4,3,2,1,0:T(8,128)}, f32[1,256,1024]{1,2,0:T(8,128)}), (f32[1,3,3,256,1024]{4,3,2,1,0:T(8,128)}, f32[1,256,1024]{1,2,0:T(8,128)})) %all-reduce.3.cloned.1.call-update) | async-done | bytes 10485776 | tf_op jit(solution)/shard_map/psum | solution.py:44
  691.3 2.5 copy.53
  693.8 9.4 %copy.72 = f32[1,3,3,256,1024]{4,3,2,1,0:T(8,128)} copy(f32[1,3,3,256,1024]{4,3,2,1,0:T(8,128)} %get-tuple-element.27) | data formatting | bytes 18874368
Async XLA Ops:
  7.2 123.3 %copy-start = (bf16[1,256,1024]{2,1,0:T(8,128)(2,1)S(1)}, bf16[1,256,1024]{2,1,0:T(8,128)(2,1)}, u32[]{:S(2)}) copy-start(bf16[1,256,1024]{2,1,0:T(8,128)(2,1)} %param.9) | copy-start | bytes 1572868
  7.2 224.5 %reduce-scatter.5.cloned.1.call-start = ((), (), s32[]{:S(2)}) async-start(), calls=%async_computation.5 | async-start | bytes 16056320 | tf_op jit(solution)/shard_map/reduce_scatter | solution.py:32
  97.4 33.1 %collective-permute-start = (bf16[12,14,14,256]{3,2,1,0:T(8,128)(2,1)S(1)}, bf16[12,14,14,256]{3,2,1,0:T(8,128)(2,1)S(1)}, u32[]{:S(2)}, u32[]{:S(2)}) collective-permute-start(bf16[12,14,14,256]{3,2,1,0:T(8,128)(2,1)S(1)} %bitcast.53), channel_id=1, source_target_pairs={{0,4},{1,5},{2,6},{3,7},{8,12},{9,13},{10,14},{11,15}} | collective-permute-start | bytes 3612680 | tf_op jit(solution)/shard_map/ppermute | solution.py:24
  137.0 191.2 %reduce-scatter.3.cloned.1.call-start = ((), (), s32[]{:S(2)}) async-start(), calls=%async_computation.4 | async-start | bytes 16056320 | tf_op jit(solution)/shard_map/reduce_scatter | solution.py:32
  156.3 171.9 %copy-start.2 = (f32[1,256]{1,0:T(1,128)S(1)}, f32[1,256]{1,0:T(1,128)}, u32[]{:S(2)}) copy-start(f32[1,256]{1,0:T(1,128)} %param.12) | copy-start | bytes 3076
  156.3 171.9 %copy-start.3 = (f32[1,256]{1,0:T(1,128)S(1)}, f32[1,256]{1,0:T(1,128)}, u32[]{:S(2)}) copy-start(f32[1,256]{1,0:T(1,128)} %param.10) | copy-start | bytes 3076
  156.3 171.9 %copy-start.4 = (f32[1,256]{1,0:T(1,128)S(1)}, f32[1,256]{1,0:T(1,128)}, u32[]{:S(2)}) copy-start(f32[1,256]{1,0:T(1,128)} %param.11) | copy-start | bytes 3076
  156.4 227.6 %all-gather.5.cloned.1.call-start = ((), (), s32[]{:S(2)}) async-start(), calls=%async_computation.7 | async-start | bytes 8028160 | tf_op jit(solution)/shard_map/all_gather | solution.py:39
  328.2 6.3 copy-start.1
  337.0 95.1 %all-gather.3.cloned.1.call-start = ((), (), s32[]{:S(2)}) async-start(), calls=%async_computation.6 | async-start | bytes 8028160 | tf_op jit(solution)/shard_map/all_gather | solution.py:39
  337.6 353.8 %all-reduce.3.cloned.1.call-start = ((), (), s32[]{:S(2)}) async-start(), calls=%async_computation.8 | async-start | bytes 20971520 | tf_op jit(solution)/shard_map/psum | solution.py:44
  477.8 31.4 %collective-permute-start.1 = (bf16[12,14,14,256]{3,2,1,0:T(8,128)(2,1)S(1)}, bf16[12,14,14,256]{3,2,1,0:T(8,128)(2,1)}, u32[]{:S(2)}, u32[]{:S(2)}) collective-permute-start(bf16[12,14,14,256]{3,2,1,0:T(8,128)(2,1)S(1)} %copy.48), channel_id=1, source_target_pairs={{4,0},{5,1},{6,2},{7,3},{12,8},{13,9},{14,10},{15,11}} | collective-permute-start | bytes 3612680 | tf_op jit(solution)/shard_map/ppermute | solution.py:45
  509.2 21.5 %all-to-all-start.1 = ((bf16[12,14,14,256]{3,2,1,0:T(8,128)(2,1)}), bf16[12,14,14,256]{3,2,1,0:T(8,128)(2,1)S(1)}, u32[]{:S(2)}, u32[]{:S(2)}) async-start(bf16[12,14,14,256]{3,2,1,0:T(8,128)(2,1)} %collective-permute-done.1), calls=%async_computation.3 | async-start | bytes 2752512 | tf_op jit(solution)/shard_map/all_to_all | solution.py:46
Sparse Core Ops, SparseCore 0:
  137.1 94.4 reduce-scatter.4
  234.2 93.9 reduce-scatter.2
  337.1 46.7 all-gather.4
  385.9 46.1 all-gather.2
  452.8 238.5 all-reduce.2
where the time goes:
time: 721 us; the launch traced here: 710 us
  waiting for transfers between devices  494 us (69%)
  local copies, waits for them, and re-layouts  87.7 us (12%)
  matrix products  76.8 us (11%)
  blocking collectives  18.8 us (3%)
  between operations  14.3 us (2%)
  starting transfers between devices  9.8 us (1%)
  other arithmetic  8.7 us (1%)
    reduce_scatter x2, waiting for transfers between devices, device_step(): lax.psum_scatter((pre_part, short_part), 'tp', scatter_dimension=3, tiled...  172 us
    psum x1, waiting for transfers between devices, device_step(): dw_sum, dws_sum = lax.psum((dw_part, dws_part), 'dp')  158 us
    all_gather x2, waiting for transfers between devices, device_step(): lax.all_gather((g_main, g_short), 'tp', axis=3, tiled=True)  88.3 us
    unnamed x17, local copies, waits for them, and re-layouts  69.7 us
    conv_general_dilated x2, matrix products, conv_same(): lax.conv_general_dilated(left_op, right_op, (1, 1), 'SAME', dimension_num...  39.2 us
    ppermute x1, waiting for transfers between devices, device_step(): act_local = lax.ppermute(by_channel, 'stage', perm=[(0, 1)])  31.8 us
    ppermute x1, waiting for transfers between devices, device_step(): returned = lax.ppermute(grad_local, 'stage', perm=[(1, 0)])  28.1 us
    conv_general_dilated x1, matrix products, weight_grad(): lax.conv_general_dilated(images_in, grads_out, (1, 1), ((1, 1), (1, 1)),...  20.6 us
  transfers between devices with their start and end apart: 8, of which 8 were waited for; matrix products, arithmetic and copies ran while one was open for 8% of the time, Pallas kernels for 0%

commit v1 on v0

v1 whole, which is shorter than its diff:
```python
import jax
import jax.numpy as jnp
from jax import lax
from jax.experimental import pallas as pl
from jax.experimental.pallas import tpu as pltpu
from jax.sharding import PartitionSpec as P

BF = jnp.bfloat16
F32 = jnp.float32
MESH = pl.DeviceIdType.MESH
ROWS = 224
HALO = 240
SET = 4 * ROWS
NT = (((1,), (1,)), ((), ()))


def dot(a, b):
    return jnp.dot(a, b, preferred_element_type=F32)


def dot_t(a, b):
    return lax.dot_general(a, b, NT, preferred_element_type=F32)


def mo(v, m):
    return pl.multiple_of(v, m)


def block_kernel(
    x0, wc, ws, vec, dz_in,
    z_out, dx_out, dw_out, ds_out,
    xa, wo, wr, vecs, dz, ga, xz, xt, gh, gsh, gx, gsx, dwa, zs, dxs,
    s_send, s_loc, r_ws, r_wx, r_wz, r_v, r_x, r_xz, r_g, r_dx,
):
    z = lax.axis_index("dp")
    st = lax.axis_index("stage")
    k = lax.axis_index("tp")
    zo = 1 - z
    k1 = k + 1 - 2 * lax.rem(k, 2)
    k2 = lax.rem(k + 2, 4)
    k3 = 3 - k

    def dev(dp=None, stage=None, tp=None):
        return (z if dp is None else dp, st if stage is None else stage, k if tp is None else tp)

    sends = []

    def send(src, dst, rsem, **to):
        c = pltpu.make_async_remote_copy(src, dst, s_send.at[len(sends)], rsem, device_id=dev(**to), device_id_type=MESH)
        c.start()
        sends.append(c)

    def recv(dst, rsem):
        pltpu.make_async_remote_copy(dst, dst, s_send.at[0], rsem, device_id=dev(), device_id_type=MESH).wait_recv()

    def image(n):
        return xa.at[pl.ds(mo((n * 15 + 1) * 16, 16), ROWS)]

    @pl.when(st == 0)
    def _():
        for i in range(3):
            send(x0.at[pl.ds(i * ROWS, ROWS)], image(i * 4 + k), r_x.at[i * 4 + k], tp=k2)
        for i in range(3):
            send(x0.at[pl.ds(i * ROWS, ROWS)], image(i * 4 + k), r_x.at[i * 4 + k], stage=1)
            recv(image(i * 4 + k2), r_x.at[i * 4 + k2])
            send(image(i * 4 + k2), image(i * 4 + k2), r_x.at[i * 4 + k2], stage=1)
        for i in range(3):
            for q in range(4):
                recv(dx_out.at[pl.ds(i * ROWS, ROWS), pl.ds(q * 256, 256)], r_dx.at[i, q])
        for c in sends:
            c.wait_send()

    sends.clear()

    @pl.when(st == 1)
    def _():
        kc = mo(k * 256, 256)

        def wsrc(tap, q):
            return wo.at[tap, :, pl.ds(mo(q * 256, 256), 256)]

        def wdst(tap, q):
            return wr.at[tap, pl.ds(mo(q * 256, 256), 256)]

        local = [
            pltpu.make_async_copy(wc, wo.at[pl.ds(0, 9)], s_loc.at[4]),
            pltpu.make_async_copy(ws, wo.at[9], s_loc.at[5]),
            pltpu.make_async_copy(vec, vecs.at[k], s_loc.at[2]),
            pltpu.make_async_copy(dz_in, dz, s_loc.at[3]),
            pltpu.make_async_copy(wc.at[:, :, pl.ds(kc, 256)], wr.at[pl.ds(0, 9), pl.ds(kc, 256)], s_loc.at[0]),
            pltpu.make_async_copy(ws.at[:, pl.ds(kc, 256)], wr.at[9, pl.ds(kc, 256)], s_loc.at[1]),
        ]
        for c in local:
            c.start()
        for c in local[:2]:
            c.wait()
        mine, other = z * 5, zo * 5
        for t in range(5):
            send(wsrc(mine + t, k2), wdst(mine + t, k), r_wx.at[0, t], tp=k2)
            send(wsrc(mine + t, k3), wdst(mine + t, k), r_wx.at[1, t], tp=k3)
        send(
            wo.at[:, :, pl.ds(mo(k1 * 256, 256), 256)], wr.at[:, pl.ds(kc, 256)], r_ws.at[0], tp=k1
        )
        for n, p in enumerate((k1, k2, k3)):
            send(vec, vecs.at[k], r_v.at[n], tp=p)

        def zero_rows(n, _):
            xa[pl.ds(mo(n * HALO, 16), 16)] = jnp.zeros((16, 1024), BF)
            return 0

        lax.fori_loop(0, 13, zero_rows, 0)
        for n in range(5):
            gx[pl.ds(n * HALO, 16)] = jnp.zeros((16, 1024), BF)
        for n in range(9):
            gh[pl.ds(n * HALO, 16)] = jnp.zeros((16, 256), BF)

        for t in range(5):
            for s, q in ((0, k2), (1, k3)):
                recv(wdst(mine + t, q), r_wx.at[s, t])
                send(wdst(mine + t, q), wdst(mine + t, q), r_wz.at[s, t], dp=zo)

        for n, p in enumerate((k1, k2, k3)):
            recv(vecs.at[p], r_v.at[n])
        for c in local[2:]:
            c.wait()

        def rows_of(b):
            return [mo((b * 2 + n) * HALO, 16) for n in range(2)]

        def fwd(i):
            gam, bet, gsc = vecs[k, 0:1, :], vecs[k, 1:2, :], vecs[k, 2:3, :]

            def body(b, _):
                bases = rows_of(i * 2 + b)

                def lhs(t):
                    return jnp.concatenate([xa[pl.ds(mo(s + t * 16, 16), ROWS)] for s in bases], axis=0)

                parts = []
                for j in range(3):
                    acc = dot(lhs(0), wr[j])
                    acc += dot(lhs(1), wr[3 + j])
                    acc += dot(lhs(2), wr[6 + j])
                    parts.append(acc)
                pre = parts[1] + pltpu.roll(parts[0], 1, 0) + pltpu.roll(parts[2], 447, 0)
                u = pre * gam + bet + dot(lhs(1), wr[9]) * gsc
                at = pl.ds(mo(i * SET + b * 448, 64), 448)
                zs[at] = jnp.maximum(u, 0.0).astype(BF)
                ga[z, k, at] = jnp.where(u > 0.0, dz[at].astype(F32), 0.0).astype(BF)
                return 0

            lax.fori_loop(0, 2, body, 0)

        def blk(zz, q, i):
            return ga.at[zz, q, pl.ds(i * SET, SET)]

        def gsend(zz, q, i, **to):
            send(blk(zz, q, i), blk(zz, q, i), r_g.at[zz, q, i], **to)

        def grecv(zz, q, i):
            recv(blk(zz, q, i), r_g.at[zz, q, i])

        def put_xt(val, t):
            v = val.astype(F32)
            for j in range(3):
                w = v if j == 1 else pltpu.roll(v, (1 - j) % SET, 0)
                xt[j, :, pl.ds(t * SET, SET)] = w.T.astype(BF)

        def dx(i):
            for q in range(4):
                gam, gsc = vecs[q, 0:1, :], vecs[q, 2:3, :]

                def scale(n, _):
                    v = ga[z, q, pl.ds(mo(i * SET + n * ROWS, 32), ROWS)].astype(F32)
                    gx[pl.ds(mo(n * HALO + 16, 16), ROWS), pl.ds(q * 256, 256)] = (v * gam).astype(BF)
                    gsx[pl.ds(mo(n * ROWS, 32), ROWS), pl.ds(q * 256, 256)] = (v * gsc).astype(BF)
                    return 0

                lax.fori_loop(0, 4, scale, 0)

            def body(b, _):
                bases = rows_of(b)

                def lhs(t):
                    return jnp.concatenate([gx[pl.ds(mo(s + (2 - t) * 16, 16), ROWS)] for s in bases], axis=0)

                parts = []
                for j in range(3):
                    acc = dot_t(lhs(0), wo[j])
                    acc += dot_t(lhs(1), wo[3 + j])
                    acc += dot_t(lhs(2), wo[6 + j])
                    parts.append(acc)
                tot = parts[1] + pltpu.roll(parts[0], 447, 0) + pltpu.roll(parts[2], 1, 0)
                tot += dot_t(gsx[pl.ds(mo(b * 448, 64), 448)], wo[9])
                dxs[pl.ds(mo(i * SET + b * 448, 64), 448)] = tot.astype(BF)
                return 0

            lax.fori_loop(0, 2, body, 0)
            for j in range(4):
                send(
                    dxs.at[pl.ds(i * SET + j * ROWS, ROWS)],
                    dx_out.at[pl.ds(i * ROWS, ROWS), pl.ds(kc, 256)],
                    r_dx.at[i, k],
                    stage=0, tp=j,
                )

        def dw(u, first, last):
            def per_q(q, _):
                gam, gsc = vecs[q, 0:1, :], vecs[q, 2:3, :]
                qc = pl.ds(mo(q * 256, 256), 256)

                def scale(n, _):
                    t = u * 8 + n
                    zz = jnp.where(t < 12, z, zo)
                    v = ga[zz, q, pl.ds(mo(lax.rem(t, 12) * ROWS, 32), ROWS)].astype(F32)
                    gh[pl.ds(mo(n * HALO + 16, 16), ROWS)] = (v * gam).astype(BF)
                    gsh[pl.ds(mo(n * ROWS, 32), ROWS)] = (v * gsc).astype(BF)
                    return 0

                lax.fori_loop(0, 8, scale, 0)
                lanes = pl.ds(u * 1792, 1792)
                for i in range(3):
                    rhs = jnp.concatenate([gh[pl.ds(n * HALO + (2 - i) * 16, ROWS)] for n in range(8)], axis=0)
                    for j in range(3):
                        d = dot(xt[j, :, lanes], rhs)
                        if first:
                            dwa[3 * i + j, :, qc] = d
                        else:
                            dwa[3 * i + j, :, qc] += d
                d = dot(xt[1, :, lanes], gsh[...])
                if first:
                    dwa[9, :, qc] = d
                else:
                    dwa[9, :, qc] += d
                if last:
                    pltpu.make_async_copy(dwa.at[pl.ds(0, 9), :, qc], dw_out.at[:, :, qc], s_loc.at[6 + q]).start()
                    pltpu.make_async_copy(dwa.at[9, :, qc], ds_out.at[:, qc], s_loc.at[10 + q]).start()
                return 0

            lax.fori_loop(0, 4, per_q, 0)

        def relay(i):
            grecv(z, k2, i)
            gsend(z, k2, i, tp=k1)
            grecv(zo, k, i)
            gsend(zo, k, i, tp=k2)
            gsend(zo, k, i, tp=k1)

        def backward(i):
            relay(i)
            grecv(z, k1, i)
            grecv(z, k3, i)
            dx(i)

        for i in range(3):
            for p in (k, k2):
                recv(image(i * 4 + p), r_x.at[i * 4 + p])
                send(image(i * 4 + p), image(i * 4 + p), r_x.at[i * 4 + p], tp=k1)
            for p in (k1, k3):
                recv(image(i * 4 + p), r_x.at[i * 4 + p])
            if i == 0:
                recv(wr.at[:, pl.ds(mo(k1 * 256, 256), 256)], r_ws.at[0])
                for t in range(5):
                    for s, q in ((0, k2), (1, k3)):
                        recv(wdst(other + t, q), r_wz.at[s, t])
            fwd(i)
            pltpu.make_async_copy(zs.at[pl.ds(i * SET, SET)], z_out.at[pl.ds(i * SET, SET)], s_loc.at[14 + i]).start()
            gsend(z, k, i, tp=k2)
            gsend(z, k, i, dp=zo)
            gsend(z, k, i, tp=k1)
            for j in range(4):
                send(
                    xa.at[pl.ds(((i * 4 + j) * 15 + 1) * 16, ROWS), pl.ds(kc, 256)],
                    xz.at[pl.ds(i * SET + j * ROWS, ROWS)],
                    r_xz.at[i, j],
                    dp=zo,
                )
            put_xt(
                jnp.concatenate(
                    [xa[pl.ds(((i * 4 + j) * 15 + 1) * 16, ROWS), pl.ds(kc, 256)] for j in range(4)], axis=0
                ),
                i,
            )
            if i > 0:
                backward(i - 1)
        dw(0, True, False)
        backward(2)
        for i in range(3):
            grecv(zo, k2, i)
            gsend(zo, k2, i, tp=k1)
            for j in range(4):
                recv(xz.at[pl.ds(i * SET + j * ROWS, ROWS)], r_xz.at[i, j])
            put_xt(xz[pl.ds(i * SET, SET)], 3 + i)
            grecv(zo, k1, i)
            grecv(zo, k3, i)
            if i != 1:
                dw(1 + i // 2, False, i == 2)
        for i in range(3):
            pltpu.make_async_copy(zs.at[pl.ds(i * SET, SET)], z_out.at[pl.ds(i * SET, SET)], s_loc.at[14 + i]).wait()
        for q in range(4):
            qc = pl.ds(q * 256, 256)
            pltpu.make_async_copy(dwa.at[pl.ds(0, 9), :, qc], dw_out.at[:, :, qc], s_loc.at[6 + q]).wait()
            pltpu.make_async_copy(dwa.at[9, :, qc], ds_out.at[:, qc], s_loc.at[10 + q]).wait()
        for c in sends:
            c.wait_send()


def solution(mesh):
    act_spec = P("stage", ("dp", "tp"), None, None, None)
    kernel_spec = P("stage", None, None, "tp", None)
    short_spec = P("stage", "tp", None)
    vec_spec = P("stage", "tp")
    grad_spec = P("stage", "dp", None, None, "tp")

    def device_step(act_in, w_conv, w_short, gamma, beta, gamma_s, grad_z):
        pads = ((0, 0), (0, 0), (0, 2), (0, 0))
        x0 = jnp.pad(act_in[0], pads).reshape(3 * ROWS, 1024)
        dz = jnp.pad(grad_z[0], pads).reshape(4, 3, ROWS, 256).transpose(1, 0, 2, 3).reshape(12 * ROWS, 256)
        vec = jnp.concatenate([gamma, beta, gamma_s, jnp.zeros((5, 256), F32)], axis=0)
        any_spec = pl.BlockSpec(memory_space=pl.ANY)
        dma = pltpu.SemaphoreType.DMA
        z, dx, dw, ds = pl.pallas_call(
            block_kernel,
            out_shape=(
                jax.ShapeDtypeStruct((12 * ROWS, 256), BF),
                jax.ShapeDtypeStruct((3 * ROWS, 1024), BF),
                jax.ShapeDtypeStruct((9, 256, 1024), F32),
                jax.ShapeDtypeStruct((256, 1024), F32),
            ),
            in_specs=[any_spec] * 5,
            out_specs=(any_spec,) * 4,
            scratch_shapes=[
                pltpu.VMEM((12 * HALO + 16, 1024), BF),
                pltpu.VMEM((10, 256, 1024), BF),
                pltpu.VMEM((10, 1024, 256), BF),
                pltpu.VMEM((4, 8, 256), F32),
                pltpu.VMEM((12 * ROWS, 256), BF),
                pltpu.VMEM((2, 4, 12 * ROWS, 256), BF),
                pltpu.VMEM((12 * ROWS, 256), BF),
                pltpu.VMEM((3, 256, 24 * ROWS), BF),
                pltpu.VMEM((8 * HALO + 16, 256), BF),
                pltpu.VMEM((8 * ROWS, 256), BF),
                pltpu.VMEM((4 * HALO + 16, 1024), BF),
                pltpu.VMEM((4 * ROWS, 1024), BF),
                pltpu.VMEM((10, 256, 1024), F32),
                pltpu.VMEM((12 * ROWS, 256), BF),
                pltpu.VMEM((12 * ROWS, 256), BF),
                dma((100,)),
                dma((20,)),
                dma((1,)),
                dma((2, 5)),
                dma((2, 5)),
                dma((3,)),
                dma((12,)),
                dma((3, 4)),
                dma((2, 4, 3)),
                dma((3, 4)),
            ],
            compiler_params=pltpu.CompilerParams(has_side_effects=True, vmem_limit_bytes=67043328),
        )(x0, w_conv[0].reshape(9, 256, 1024), w_short[0], vec, dz)
        on = lax.axis_index("stage") == 1
        z = z.reshape(3, 4, 14, 16, 256).transpose(1, 0, 2, 3, 4).reshape(12, 14, 16, 256)[:, :, :14]
        z = jnp.where(on, z, jnp.zeros_like(z))
        dx = dx.reshape(3, 14, 16, 1024)[:, :, :14]
        dx = jnp.where(on, jnp.zeros_like(dx), dx)
        dw = jnp.where(on, dw, 0.0).reshape(1, 3, 3, 256, 1024)
        ds = jnp.where(on, ds, 0.0)
        return z[None], dx[None], dw, ds[None]

    return jax.shard_map(device_step, mesh=mesh, in_specs=(act_spec, kernel_spec, short_spec, vec_spec, vec_spec, vec_spec, grad_spec), out_specs=(grad_spec, act_spec, kernel_spec, short_spec), check_vma=False)
```

time: 721 us -> 156 us (0.22); the launches traced: 710 us -> 156 us
  waiting for transfers between devices: 494 us -> 0 us
  Pallas kernels: 0 us -> 137 us
  local copies, waits for them, and re-layouts: 87.7 us -> 5.84 us
  matrix products: 76.8 us -> 0 us
  blocking collectives: 18.8 us -> 0 us
  between operations: 14.3 us -> 0.68 us
  starting transfers between devices: 9.8 us -> 0 us
    reduce_scatter x2 -> x0, waiting for transfers between devices: 172 us -> none  [device_step(): lax.psum_scatter((pre_part, short_part), 'tp', scatter_dimension=3, tiled...]
    psum x1 -> x0, waiting for transfers between devices: 158 us -> none  [device_step(): dw_sum, dws_sum = lax.psum((dw_part, dws_part), 'dp')]
    pallas_call x0 -> x1, Pallas kernels: none -> 137 us  [device_step(): pl.pallas_call(block_kernel, out_shape=(jax.ShapeDtypeStruct((12 * ROWS,...]
    all_gather x2 -> x0, waiting for transfers between devices: 88.3 us -> none  [device_step(): lax.all_gather((g_main, g_short), 'tp', axis=3, tiled=True)]
    unnamed x17 -> x4, local copies, waits for them, and re-layouts: 69.7 us -> 0.01 us
    ppermute x2 -> x0, waiting for transfers between devices: 59.9 us -> none  [the longest x1 31.8 us: device_step(): act_local = lax.ppermute(by_channel, 'stage', perm=[(0, 1)])]
    conv_general_dilated x3 -> x0, matrix products: 59.7 us -> none  [the longest x2 39.2 us: conv_same(): lax.conv_general_dilated(left_op, right_op, (1, 1), 'SAME', dimension_num...]
    all_to_all x1 -> x0, blocking collectives: 18.8 us -> none  [device_step(): by_channel = lax.all_to_all(act_in[0], 'tp', 3, 0, tiled=True)]
  transfers between devices with their start and end apart: 8 -> 0, of which waited for: 8 -> 0; matrix products, arithmetic and copies ran while one was open for 8% -> 0% of each run, Pallas kernels for 0% -> 0%
where the time goes in v1:
time: 156 us
  Pallas kernels  137 us (88%)
  other arithmetic  13 us (8%)
  local copies, waits for them, and re-layouts  5.84 us (4%)
    pallas_call x1, Pallas kernels, device_step(): pl.pallas_call(block_kernel, out_shape=(jax.ShapeDtypeStruct((12 * ROWS,...  137 us
    broadcast_in_dim x3, other arithmetic, device_step(): return (z[None], dx[None], dw, ds[None])  6.73 us
    select_n x1, other arithmetic, device_step(): dw = jnp.where(on, dw, 0.0).reshape(1, 3, 3, 256, 1024)  4.85 us

profile of v1, /device:TPU:5, one launch (start us, length us, event | category | flops | bytes accessed | tf_op | source)
XLA Modules:
  0.0 156.1 jit_solution(8179100210228904233)
XLA Ops:
  0.6 0.1 pad.13.clone
  0.7 1.4 maximum_maximum_fusion.vec
  2.1 0.0 copy-start.1
  2.1 2.8 %pad.8 = bf16[3,14,16,1024]{3,2,1,0:T(8,128)(2,1)} pad(bf16[3,14,14,1024]{3,2,1,0:T(8,128)(2,1)} %bitcast.27, bf16[]{:T(256)} %constant.3.clone.1), padding=0_0x0_0x0_2x0_0 | pad | bytes 2580482 | tf_op jit(solution)/shard_map/jit(_pad)/pad | solution.py:317
  4.9 0.0 copy-done.1
  4.9 0.2 pad.9
  5.1 1.2 copy.11
  6.3 136.6 %shard_map.102 = (bf16[2688,256]{1,0:T(8,128)(2,1)}, bf16[672,1024]{1,0:T(8,128)(2,1)}, f32[9,256,1024]{2,1,0:T(8,128)}, f32[256,1024]{1,0:T(8,128)}) custom-call(bf16[672,1024]{1,0:T(8,128)(2,1)} %bitcast.24, bf16[9,256,1024]{2,1,0:T(8,128)(2,1)} %bitcast.26, bf16[256,1024]{1,0:T(8,128)(2,1)} %bitcast.31, f32[8,256]{1,0:T(8,128)} %maximum_maximum_fusion.vec, ...), custom_call_target="tpu_custom_call" | custom-call | tf_op jit(solution)/shard_map/pallas_call | solution.py:322
  142.9 0.0 copy-start
  142.9 1.6 %copy.12 = bf16[4,3,14,16,256]{4,3,2,1,0:T(8,128)(2,1)S(1)} copy(bf16[4,3,14,16,256]{4,3,2,0,1:T(8,128)(2,1)} %bitcast.30) | data formatting | bytes 2752512 | tf_op jit(solution)/shard_map/transpose | solution.py:362
  144.5 1.2 fusion.1
  145.7 3.3 %fusion = bf16[1,3,14,14,1024]{4,3,2,1,0:T(8,128)(2,1)} fusion(bf16[3,14,16,1024]{3,2,1,0:T(8,128)(2,1)} %bitcast.29, pred[]{:T(512)S(6)} %eq.3), kind=kLoop, calls=%fused_computation.2 | loop fusion | flops 602112 | bytes 2408449 | tf_op jit(solution)/shard_map/broadcast_in_dim | solution.py:368
  148.9 2.3 %select_bitcast_fusion = f32[1,256,1024]{2,1,0:T(8,128)} fusion(f32[256,1024]{1,0:T(8,128)} %get-tuple-element.11, pred[]{:T(512)S(6)} %eq.3), kind=kLoop, calls=%fused_computation.5 | loop fusion | flops 262144 | bytes 2097153 | tf_op jit(solution)/shard_map/broadcast_in_dim | solution.py:368
  151.2 0.0 copy-done
  151.2 4.8 %broadcast_select_fusion = f32[9,256,1024]{2,1,0:T(8,128)} fusion(f32[9,256,1024]{2,1,0:T(8,128)S(1)} %copy-done, pred[]{:T(512)S(6)} %eq.3), kind=kLoop, calls=%fused_computation | loop fusion | flops 2359296 | bytes 18874368 | tf_op jit(solution)/shard_map/jit(_where)/select_n | solution.py:366
  (1 shorter events, 0.0 us)
Async XLA Ops:
  2.1 2.8 %copy-start.1 = (bf16[1,12,14,14,256]{4,3,2,1,0:T(8,128)(2,1)S(1)}, bf16[1,12,14,14,256]{4,3,2,1,0:T(8,128)(2,1)}, u32[]{:S(2)}) copy-start(bf16[1,12,14,14,256]{4,3,2,1,0:T(8,128)(2,1)} %param.13) | copy-start | bytes 3612676
  142.9 8.3 %copy-start = (f32[9,256,1024]{2,1,0:T(8,128)S(1)}, f32[9,256,1024]{2,1,0:T(8,128)}, u32[]{:S(2)}) copy-start(f32[9,256,1024]{2,1,0:T(8,128)} %get-tuple-element.10) | copy-start | bytes 28311556

commit v2 on v1

--- a/solution.py
+++ b/solution.py
@@ -27,10 +27,10 @@
 
 
 def block_kernel(
-    x0, wc, ws, vec, dz_in,
+    act, wc, ws, gam_in, gs_in, bet, dz_in,
     z_out, dx_out, dw_out, ds_out,
-    xa, wo, wr, vecs, dz, ga, xz, xt, gh, gsh, gx, gsx, dwa, zs, dxs,
-    s_send, s_loc, r_ws, r_wx, r_wz, r_v, r_x, r_xz, r_g, r_dx,
+    xa, wo, wr, gamv, gsv, dz, ga, xz, xt, gh, gsh, gx, gsx, dwa, zs, dxs, a14,
+    s_send, s_loc, r_ws, r_wx, r_wz, r_v, r_x, r_xs, r_xz, r_g, r_dx,
 ):
     z = lax.axis_index("dp")
     st = lax.axis_index("stage")
@@ -56,17 +56,64 @@
     def image(n):
         return xa.at[pl.ds(mo((n * 15 + 1) * 16, 16), ROWS)]
 
+    def img_rows(i, j):
+        return pl.ds(mo((i * 4 + j) * ROWS, 32), ROWS)
+
+    def zcols(q):
+        return pl.ds(mo(q * 256, 256), 256)
+
     @pl.when(st == 0)
     def _():
-        for i in range(3):
-            send(x0.at[pl.ds(i * ROWS, ROWS)], image(i * 4 + k), r_x.at[i * 4 + k], tp=k2)
-        for i in range(3):
-            send(x0.at[pl.ds(i * ROWS, ROWS)], image(i * 4 + k), r_x.at[i * 4 + k], stage=1)
-            recv(image(i * 4 + k2), r_x.at[i * 4 + k2])
-            send(image(i * 4 + k2), image(i * 4 + k2), r_x.at[i * 4 + k2], stage=1)
+        loads = [pltpu.make_async_copy(act.at[i], a14.at[i], s_loc.at[i]) for i in range(3)]
+        for c in loads:
+            c.start()
+        qa = 2 * (k // 2)
+
+        def to_z(i, j):
+            for n in range(2):
+                src = xa.at[pl.ds(mo(((i * 4 + j) * 15 + 1) * 16, 16), ROWS), zcols(qa + n)]
+                send(src, ga.at[0, qa + n, img_rows(i, j)], r_xs.at[i * 4 + j, n], dp=zo)
+
+        def y_image(i, j):
+            send(image(i * 4 + j), image(i * 4 + j), r_x.at[i * 4 + j], stage=1)
+
+        for i in range(3):
+            loads[i].wait()
+
+            def pad(h, _):
+                row = ((i * 4 + k) * 15 + 1 + h) * 16
+                xa[pl.ds(mo(row, 16), 16)] = jnp.concatenate([a14[i, h], jnp.zeros((2, 1024), BF)], axis=0)
+                return 0
+
+            lax.fori_loop(0, 14, pad, 0)
+            if i != 1:
+                send(image(i * 4 + k), image(i * 4 + k), r_x.at[i * 4 + k], tp=k2)
+            if i < 2:
+                y_image(i, k)
+        send(image(4 + k), image(4 + k), r_x.at[4 + k], tp=k2)
+        for i in range(3):
+            to_z(i, k)
+        recv(image(k2), r_x.at[k2])
+        y_image(0, k2)
+        y_image(2, k)
+        recv(image(8 + k2), r_x.at[8 + k2])
+        y_image(2, k2)
+        recv(image(4 + k2), r_x.at[4 + k2])
+        for i in range(3):
+            to_z(i, k2)
+        for i in range(3):
+            for j in (k, k2):
+                for n in range(2):
+                    buf = ga.at[0, qa + n, img_rows(i, j)]
+                    recv(buf, r_xs.at[i * 4 + j, n])
+                    send(buf, xz.at[img_rows(i, j)], r_xz.at[i, j], stage=1, tp=qa + n)
+        zs[...] = jnp.zeros((12, 14, 14, 256), BF)
+        fill = pltpu.make_async_copy(zs, z_out, s_loc.at[0])
+        fill.start()
+        fill.wait()
         for i in range(3):
             for q in range(4):
-                recv(dx_out.at[pl.ds(i * ROWS, ROWS), pl.ds(q * 256, 256)], r_dx.at[i, q])
+                recv(dx_out.at[i, :, :, pl.ds(q * 256, 256)], r_dx.at[i, q])
         for c in sends:
             c.wait_send()
 
@@ -85,8 +132,9 @@
         local = [
             pltpu.make_async_copy(wc, wo.at[pl.ds(0, 9)], s_loc.at[4]),
             pltpu.make_async_copy(ws, wo.at[9], s_loc.at[5]),
-            pltpu.make_async_copy(vec, vecs.at[k], s_loc.at[2]),
-            pltpu.make_async_copy(dz_in, dz, s_loc.at[3]),
+            pltpu.make_async_copy(gam_in, gamv.at[k], s_loc.at[2]),
+            pltpu.make_async_copy(gs_in, gsv.at[k], s_loc.at[18]),
+            pltpu.make_async_copy(dz_in, zs, s_loc.at[3]),
             pltpu.make_async_copy(wc.at[:, :, pl.ds(kc, 256)], wr.at[pl.ds(0, 9), pl.ds(kc, 256)], s_loc.at[0]),
             pltpu.make_async_copy(ws.at[:, pl.ds(kc, 256)], wr.at[9, pl.ds(kc, 256)], s_loc.at[1]),
         ]
@@ -102,7 +150,8 @@
             wo.at[:, :, pl.ds(mo(k1 * 256, 256), 256)], wr.at[:, pl.ds(kc, 256)], r_ws.at[0], tp=k1
         )
         for n, p in enumerate((k1, k2, k3)):
-            send(vec, vecs.at[k], r_v.at[n], tp=p)
+            send(gam_in, gamv.at[k], r_v.at[n, 0], tp=p)
+            send(gs_in, gsv.at[k], r_v.at[n, 1], tp=p)
 
         def zero_rows(n, _):
             xa[pl.ds(mo(n * HALO, 16), 16)] = jnp.zeros((16, 1024), BF)
@@ -114,21 +163,53 @@
         for n in range(9):
             gh[pl.ds(n * HALO, 16)] = jnp.zeros((16, 256), BF)
 
+        dxs[...] = jnp.zeros((12, 14, 14, 256), BF)
+        for c in local[2:]:
+            c.wait()
+        fills = [
+            pltpu.make_async_copy(dxs.at[pl.ds(0, 3)], dx_out.at[:, :, :, zcols(q)], s_loc.at[6 + q]) for q in range(4)
+        ]
+        for c in fills:
+            c.start()
+
+        def pad_dz(r, _):
+            n, h = r // 14, lax.rem(r, 14)
+            j, i = n // 3, lax.rem(n, 3)
+            row = (i * 4 + j) * ROWS + h * 16
+            dz[pl.ds(mo(row, 16), 16)] = jnp.concatenate([zs[n, h], jnp.zeros((2, 256), BF)], axis=0)
+            return 0
+
+        lax.fori_loop(0, 168, pad_dz, 0)
+        for c in fills:
+            c.wait()
+
+        def forward_image(i, j, **to):
+            send(image(i * 4 + j), image(i * 4 + j), r_x.at[i * 4 + j], **to)
+
+        def take(i, j):
+            recv(image(i * 4 + j), r_x.at[i * 4 + j])
+
         for t in range(5):
             for s, q in ((0, k2), (1, k3)):
                 recv(wdst(mine + t, q), r_wx.at[s, t])
                 send(wdst(mine + t, q), wdst(mine + t, q), r_wz.at[s, t], dp=zo)
+            if t == 1:
+                take(0, k)
+                forward_image(0, k, tp=k1)
+            if t == 3:
+                take(1, k)
+                forward_image(1, k, tp=k2)
+                forward_image(1, k, tp=k1)
 
         for n, p in enumerate((k1, k2, k3)):
-            recv(vecs.at[p], r_v.at[n])
-        for c in local[2:]:
-            c.wait()
+            recv(gamv.at[p], r_v.at[n, 0])
+            recv(gsv.at[p], r_v.at[n, 1])
 
         def rows_of(b):
             return [mo((b * 2 + n) * HALO, 16) for n in range(2)]
 
         def fwd(i):
-            gam, bet, gsc = vecs[k, 0:1, :], vecs[k, 1:2, :], vecs[k, 2:3, :]
+            gam, beta, gsc = gamv[k], bet[...], gsv[k]
 
             def body(b, _):
                 bases = rows_of(i * 2 + b)
@@ -143,9 +224,12 @@
                     acc += dot(lhs(2), wr[6 + j])
                     parts.append(acc)
                 pre = parts[1] + pltpu.roll(parts[0], 1, 0) + pltpu.roll(parts[2], 447, 0)
-                u = pre * gam + bet + dot(lhs(1), wr[9]) * gsc
+                u = pre * gam + beta + dot(lhs(1), wr[9]) * gsc
                 at = pl.ds(mo(i * SET + b * 448, 64), 448)
-                zs[at] = jnp.maximum(u, 0.0).astype(BF)
+                zb = jnp.maximum(u, 0.0).astype(BF)
+                for n in range(2):
+                    for h in range(14):
+                        zs[(b * 2 + n) * 3 + i, h] = zb[(n * 14 + h) * 16:(n * 14 + h) * 16 + 14]
                 ga[z, k, at] = jnp.where(u > 0.0, dz[at].astype(F32), 0.0).astype(BF)
                 return 0
 
@@ -168,7 +252,7 @@
 
         def dx(i):
             for q in range(4):
-                gam, gsc = vecs[q, 0:1, :], vecs[q, 2:3, :]
+                gam, gsc = gamv[q], gsv[q]
 
                 def scale(n, _):
                     v = ga[z, q, pl.ds(mo(i * SET + n * ROWS, 32), ROWS)].astype(F32)
@@ -192,21 +276,29 @@
                     parts.append(acc)
                 tot = parts[1] + pltpu.roll(parts[0], 447, 0) + pltpu.roll(parts[2], 1, 0)
                 tot += dot_t(gsx[pl.ds(mo(b * 448, 64), 448)], wo[9])
-                dxs[pl.ds(mo(i * SET + b * 448, 64), 448)] = tot.astype(BF)
+                db = tot.astype(BF)
+                for n in range(2):
+                    for h in range(14):
+                        dxs[i * 4 + b * 2 + n, h] = db[(n * 14 + h) * 16:(n * 14 + h) * 16 + 14]
                 return 0
 
             lax.fori_loop(0, 2, body, 0)
             for j in range(4):
                 send(
-                    dxs.at[pl.ds(i * SET + j * ROWS, ROWS)],
-                    dx_out.at[pl.ds(i * ROWS, ROWS), pl.ds(kc, 256)],
+                    dxs.at[i * 4 + j],
+                    dx_out.at[i, :, :, pl.ds(kc, 256)],
                     r_dx.at[i, k],
                     stage=0, tp=j,
                 )
 
-        def dw(u, first, last):
-            def per_q(q, _):
-                gam, gsc = vecs[q, 0:1, :], vecs[q, 2:3, :]
+        def quarter(n):
+            b = lax.rem(k + 2 * (n // 2), 4)
+            return b + lax.rem(n, 2) * (1 - 2 * lax.rem(b, 2))
+
+        def dw(u, first, last, lo=0, hi=4):
+            def per_q(nq, _):
+                q = quarter(nq)
+                gam, gsc = gamv[q], gsv[q]
                 qc = pl.ds(mo(q * 256, 256), 256)
 
                 def scale(n, _):
@@ -233,57 +325,77 @@
                 else:
                     dwa[9, :, qc] += d
                 if last:
-                    pltpu.make_async_copy(dwa.at[pl.ds(0, 9), :, qc], dw_out.at[:, :, qc], s_loc.at[6 + q]).start()
-                    pltpu.make_async_copy(dwa.at[9, :, qc], ds_out.at[:, qc], s_loc.at[10 + q]).start()
+                    pltpu.make_async_copy(dwa.at[pl.ds(0, 9), :, qc], dw_out.at[:, :, qc], s_loc.at[6 + nq]).start()
+                    pltpu.make_async_copy(dwa.at[9, :, qc], ds_out.at[:, qc], s_loc.at[10 + nq]).start()
                 return 0
 
-            lax.fori_loop(0, 4, per_q, 0)
-
-        def relay(i):
-            grecv(z, k2, i)
-            gsend(z, k2, i, tp=k1)
-            grecv(zo, k, i)
-            gsend(zo, k, i, tp=k2)
-            gsend(zo, k, i, tp=k1)
-
-        def backward(i):
-            relay(i)
-            grecv(z, k1, i)
-            grecv(z, k3, i)
-            dx(i)
-
-        for i in range(3):
-            for p in (k, k2):
-                recv(image(i * 4 + p), r_x.at[i * 4 + p])
-                send(image(i * 4 + p), image(i * 4 + p), r_x.at[i * 4 + p], tp=k1)
-            for p in (k1, k3):
-                recv(image(i * 4 + p), r_x.at[i * 4 + p])
-            if i == 0:
-                recv(wr.at[:, pl.ds(mo(k1 * 256, 256), 256)], r_ws.at[0])
-                for t in range(5):
-                    for s, q in ((0, k2), (1, k3)):
-                        recv(wdst(other + t, q), r_wz.at[s, t])
+            lax.fori_loop(lo, hi, per_q, 0)
+
+        def collect(i):
+            for j in (k1, k3):
+                take(i, j)
+
+        def forward(i):
             fwd(i)
-            pltpu.make_async_copy(zs.at[pl.ds(i * SET, SET)], z_out.at[pl.ds(i * SET, SET)], s_loc.at[14 + i]).start()
             gsend(z, k, i, tp=k2)
             gsend(z, k, i, dp=zo)
             gsend(z, k, i, tp=k1)
-            for j in range(4):
-                send(
-                    xa.at[pl.ds(((i * 4 + j) * 15 + 1) * 16, ROWS), pl.ds(kc, 256)],
-                    xz.at[pl.ds(i * SET + j * ROWS, ROWS)],
-                    r_xz.at[i, j],
-                    dp=zo,
-                )
             put_xt(
                 jnp.concatenate(
                     [xa[pl.ds(((i * 4 + j) * 15 + 1) * 16, ROWS), pl.ds(kc, 256)] for j in range(4)], axis=0
                 ),
                 i,
             )
-            if i > 0:
-                backward(i - 1)
-        dw(0, True, False)
+
+        def relay_x(i):
+            grecv(z, k2, i)
+            gsend(z, k2, i, tp=k1)
+            if i == 1:
+                gsend(z, k2, i, dp=zo)
+
+        def relay_z(i):
+            grecv(zo, k, i)
+            if i != 1:
+                gsend(zo, k, i, tp=k2)
+            gsend(zo, k, i, tp=k1)
+
+        def backward(i):
+            grecv(z, k3, i)
+            dx(i)
+
+        take(0, k2)
+        forward_image(0, k2, tp=k1)
+        collect(0)
+        recv(wr.at[:, pl.ds(mo(k1 * 256, 256), 256)], r_ws.at[0])
+        for t in range(5):
+            for s, q in ((0, k2), (1, k3)):
+                recv(wdst(other + t, q), r_wz.at[s, t])
+        forward(0)
+        take(1, k2)
+        forward_image(1, k2, tp=k1)
+        take(2, k)
+        forward_image(2, k, tp=k1)
+        collect(1)
+        forward(1)
+        grecv(z, k1, 0)
+        grecv(z, k1, 1)
+        relay_x(0)
+        relay_z(0)
+        dw(0, True, False, 0, 2)
+        take(2, k2)
+        forward_image(2, k2, tp=k1)
+        collect(2)
+        forward(2)
+        relay_x(1)
+        relay_z(1)
+        backward(0)
+        backward(1)
+        zcopy = pltpu.make_async_copy(zs, z_out, s_loc.at[14])
+        zcopy.start()
+        relay_x(2)
+        relay_z(2)
+        dw(0, True, False, 2, 4)
+        grecv(z, k1, 2)
         backward(2)
         for i in range(3):
             grecv(zo, k2, i)
@@ -295,12 +407,11 @@
             grecv(zo, k3, i)
             if i != 1:
                 dw(1 + i // 2, False, i == 2)
-        for i in range(3):
-            pltpu.make_async_copy(zs.at[pl.ds(i * SET, SET)], z_out.at[pl.ds(i * SET, SET)], s_loc.at[14 + i]).wait()
-        for q in range(4):
-            qc = pl.ds(q * 256, 256)
-            pltpu.make_async_copy(dwa.at[pl.ds(0, 9), :, qc], dw_out.at[:, :, qc], s_loc.at[6 + q]).wait()
-            pltpu.make_async_copy(dwa.at[9, :, qc], ds_out.at[:, qc], s_loc.at[10 + q]).wait()
+        zcopy.wait()
+        for n in range(4):
+            qc = zcols(quarter(n))
+            pltpu.make_async_copy(dwa.at[pl.ds(0, 9), :, qc], dw_out.at[:, :, qc], s_loc.at[6 + n]).wait()
+            pltpu.make_async_copy(dwa.at[9, :, qc], ds_out.at[:, qc], s_loc.at[10 + n]).wait()
         for c in sends:
             c.wait_send()
 
@@ -313,27 +424,24 @@
     grad_spec = P("stage", "dp", None, None, "tp")
 
     def device_step(act_in, w_conv, w_short, gamma, beta, gamma_s, grad_z):
-        pads = ((0, 0), (0, 0), (0, 2), (0, 0))
-        x0 = jnp.pad(act_in[0], pads).reshape(3 * ROWS, 1024)
-        dz = jnp.pad(grad_z[0], pads).reshape(4, 3, ROWS, 256).transpose(1, 0, 2, 3).reshape(12 * ROWS, 256)
-        vec = jnp.concatenate([gamma, beta, gamma_s, jnp.zeros((5, 256), F32)], axis=0)
         any_spec = pl.BlockSpec(memory_space=pl.ANY)
         dma = pltpu.SemaphoreType.DMA
         z, dx, dw, ds = pl.pallas_call(
             block_kernel,
             out_shape=(
-                jax.ShapeDtypeStruct((12 * ROWS, 256), BF),
-                jax.ShapeDtypeStruct((3 * ROWS, 1024), BF),
+                jax.ShapeDtypeStruct((12, 14, 14, 256), BF),
+                jax.ShapeDtypeStruct((3, 14, 14, 1024), BF),
                 jax.ShapeDtypeStruct((9, 256, 1024), F32),
                 jax.ShapeDtypeStruct((256, 1024), F32),
             ),
-            in_specs=[any_spec] * 5,
+            in_specs=[any_spec] * 5 + [pl.BlockSpec(memory_space=pltpu.VMEM), any_spec],
             out_specs=(any_spec,) * 4,
             scratch_shapes=[
                 pltpu.VMEM((12 * HALO + 16, 1024), BF),
                 pltpu.VMEM((10, 256, 1024), BF),
                 pltpu.VMEM((10, 1024, 256), BF),
-                pltpu.VMEM((4, 8, 256), F32),
+                pltpu.VMEM((4, 1, 256), F32),
+                pltpu.VMEM((4, 1, 256), F32),
                 pltpu.VMEM((12 * ROWS, 256), BF),
                 pltpu.VMEM((2, 4, 12 * ROWS, 256), BF),
                 pltpu.VMEM((12 * ROWS, 256), BF),
@@ -343,26 +451,24 @@
                 pltpu.VMEM((4 * HALO + 16, 1024), BF),
                 pltpu.VMEM((4 * ROWS, 1024), BF),
                 pltpu.VMEM((10, 256, 1024), F32),
-                pltpu.VMEM((12 * ROWS, 256), BF),
-                pltpu.VMEM((12 * ROWS, 256), BF),
+                pltpu.VMEM((12, 14, 14, 256), BF),
+                pltpu.VMEM((12, 14, 14, 256), BF),
+                pltpu.VMEM((3, 14, 14, 1024), BF),
                 dma((100,)),
                 dma((20,)),
                 dma((1,)),
                 dma((2, 5)),
                 dma((2, 5)),
-                dma((3,)),
+                dma((3, 2)),
                 dma((12,)),
+                dma((12, 2)),
                 dma((3, 4)),
                 dma((2, 4, 3)),
                 dma((3, 4)),
             ],
             compiler_params=pltpu.CompilerParams(has_side_effects=True, vmem_limit_bytes=67043328),
-        )(x0, w_conv[0].reshape(9, 256, 1024), w_short[0], vec, dz)
+        )(act_in[0], w_conv[0].reshape(9, 256, 1024), w_short[0], gamma, gamma_s, beta, grad_z[0])
         on = lax.axis_index("stage") == 1
-        z = z.reshape(3, 4, 14, 16, 256).transpose(1, 0, 2, 3, 4).reshape(12, 14, 16, 256)[:, :, :14]
-        z = jnp.where(on, z, jnp.zeros_like(z))
-        dx = dx.reshape(3, 14, 16, 1024)[:, :, :14]
-        dx = jnp.where(on, jnp.zeros_like(dx), dx)
         dw = jnp.where(on, dw, 0.0).reshape(1, 3, 3, 256, 1024)
         ds = jnp.where(on, ds, 0.0)
         return z[None], dx[None], dw, ds[None]

time: 156 us -> 150 us (0.962)
  Pallas kernels: 137 us -> 134 us
  local copies, waits for them, and re-layouts: 5.84 us -> 2.91 us
    select_n x1, other arithmetic: 4.85 us -> 9.7 us  [device_step(): dw = jnp.where(on, dw, 0.0).reshape(1, 3, 3, 256, 1024)]
    broadcast_in_dim x3 -> x1, other arithmetic: 6.73 us -> 2.32 us  [device_step(): return (z[None], dx[None], dw, ds[None])]
    pad x2 -> x0, local copies, waits for them, and re-layouts: 3 us -> none  [the longest x1 2.82 us: device_step(): x0 = jnp.pad(act_in[0], pads).reshape(3 * ROWS, 1024)]
    unnamed x4 -> x6, local copies, waits for them, and re-layouts: 0.01 us -> 2.91 us
    pallas_call x1, Pallas kernels: 137 us -> 134 us  [device_step(): pl.pallas_call(block_kernel, out_shape=(jax.ShapeDtypeStruct((12, 14, 14,...]
    transpose x1 -> x0, local copies, waits for them, and re-layouts: 1.58 us -> none  [device_step(): z.reshape(3, 4, 14, 16, 256).transpose(1, 0, 2, 3, 4)]
where the time goes in v2:
time: 150 us
  Pallas kernels  134 us (89%)
  other arithmetic  12 us (8%)
  local copies, waits for them, and re-layouts  2.91 us (2%)
    pallas_call x1, Pallas kernels, device_step(): pl.pallas_call(block_kernel, out_shape=(jax.ShapeDtypeStruct((12, 14, 14,...  134 us
    select_n x1, other arithmetic, device_step(): dw = jnp.where(on, dw, 0.0).reshape(1, 3, 3, 256, 1024)  9.7 us

profile of v2, /device:TPU:5, one launch (start us, length us, event | category | flops | bytes accessed | tf_op | source)
XLA Modules:
  0.0 150.0 jit_solution(2845797068935123683)
XLA Ops:
  0.6 134.4 %shard_map.102 = (bf16[12,14,14,256]{3,2,1,0:T(8,128)(2,1)}, bf16[3,14,14,1024]{3,2,1,0:T(8,128)(2,1)}, f32[9,256,1024]{2,1,0:T(8,128)}, f32[256,1024]{1,0:T(8,128)}) custom-call(bf16[3,14,14,1024]{3,2,1,0:T(8,128)(2,1)} %bitcast.11, bf16[9,256,1024]{2,1,0:T(8,128)(2,1)} %bitcast.10, bf16[256,1024]{1,0:T(8,128)(2,1)} %bitcast.15, f32[1,256]{1,0:T(1,128)} %gam_in.1, ...), custom_call_target="tpu_custom_call" | custom-call | tf_op jit(solution)/shard_map/pallas_call | solution.py:429
  135.0 2.3 %select_bitcast_fusion = f32[1,256,1024]{2,1,0:T(8,128)} fusion(f32[256,1024]{1,0:T(8,128)} %get-tuple-element.11, pred[]{:T(512)S(6)} %eq.3), kind=kLoop, calls=%fused_computation.1 | loop fusion | flops 262144 | bytes 2097153 | tf_op jit(solution)/shard_map/broadcast_in_dim | solution.py:474
  137.3 0.0 copy-start.1
  137.3 9.7 %broadcast_select_fusion = f32[9,256,1024]{2,1,0:T(8,128)} fusion(f32[9,256,1024]{2,1,0:T(8,128)} %get-tuple-element.10, pred[]{:T(512)S(6)} %eq.3), kind=kLoop, calls=%fused_computation | loop fusion | flops 2359296 | bytes 18874368 | tf_op jit(solution)/shard_map/jit(_where)/select_n | solution.py:472
  147.1 0.0 copy-start
  147.1 0.0 copy-done.1
  147.1 1.1 copy.13
  148.1 0.8 copy-done
  148.9 1.1 copy.14
Async XLA Ops:
  137.3 9.7 %copy-start.1 = (bf16[12,14,14,256]{3,2,1,0:T(8,128)(2,1)S(1)}, bf16[12,14,14,256]{3,2,1,0:T(8,128)(2,1)}, u32[]{:S(2)}) copy-start(bf16[12,14,14,256]{3,2,1,0:T(8,128)(2,1)} %get-tuple-element.8) | copy-start | bytes 3612676
  147.1 1.8 %copy-start = (bf16[3,14,14,1024]{3,2,1,0:T(8,128)(2,1)S(1)}, bf16[3,14,14,1024]{3,2,1,0:T(8,128)(2,1)}, u32[]{:S(2)}) copy-start(bf16[3,14,14,1024]{3,2,1,0:T(8,128)(2,1)} %get-tuple-element.9) | copy-start | bytes 3612676

commit v3 on v0

v3 whole, which is shorter than its diff:
```python
import jax
import jax.numpy as jnp
from jax import lax
from jax.experimental import pallas as pl
from jax.experimental.pallas import tpu as pltpu
from jax.sharding import PartitionSpec as P

BF = jnp.bfloat16
F32 = jnp.float32
MESH = pl.DeviceIdType.MESH
PARTS = 4
LANES = 256
CHANNELS = 1024
WIDE = 16
SIDE = 14
TAPS = 9
IMAGES = 12
PAIR = 448
ROWS = 224
HALO = 240
SET = 4 * ROWS
UNIT = 8 * ROWS
NT = (((1,), (1,)), ((), ()))


def dot(a, b):
    return jnp.dot(a, b, preferred_element_type=F32)


def dot_t(a, b):
    return lax.dot_general(a, b, NT, preferred_element_type=F32)


def mo(v, m):
    return pl.multiple_of(v, m)


def zcols(q):
    return pl.ds(mo(q * LANES, LANES), LANES)


def scale_block(value, gam, gsc, gh, gsh):
    for n in range(8):
        v = value(n).astype(F32)
        gh[n * HALO + WIDE:n * HALO + HALO] = (v * gam).astype(BF)
        gsh[n * ROWS:n * ROWS + ROWS] = (v * gsc).astype(BF)


def weight_dots(xt, lanes, gh, gsh, put):
    for i in range(3):
        rhs = jnp.concatenate([gh[n * HALO + (2 - i) * WIDE:n * HALO + (2 - i) * WIDE + ROWS] for n in range(8)], axis=0)
        for j in range(3):
            put(3 * i + j, dot(xt[j, :, lanes], rhs))
    put(TAPS, dot(xt[1, :, lanes], gsh[...]))


def block_kernel(
    act, wc, ws, gam_in, gs_in, bet, dz_in,
    z_out, dx_out, acc_out, xt_out, g_out, gam_out, gs_out,
    xa, wo, wr, gamv, gsv, dz, ga, xz, xt, gh0, gsh0, gh1, gsh1, gx, gsx, dwa, zs, dxs,
    s_send, s_loc, s_tail, r_ws, r_wx, r_wz, r_v, r_x, r_xs, r_xz, r_g, r_dx, r_rel, r_h,
):
    z = lax.axis_index("dp")
    st = lax.axis_index("stage")
    k = lax.axis_index("tp")
    zo = 1 - z
    k1 = k + 1 - 2 * lax.rem(k, 2)
    k2 = lax.rem(k + 2, PARTS)
    k3 = 3 - k
    kx = k // 2
    qa = 2 * kx
    kc = mo(k * LANES, LANES)

    def dev(dp=None, stage=None, tp=None):
        return (z if dp is None else dp, st if stage is None else stage, k if tp is None else tp)

    sends = []

    def remote(src, dst, ssem, rsem, **to):
        return pltpu.make_async_remote_copy(src, dst, ssem, rsem, device_id=dev(**to), device_id_type=MESH)

    def send(src, dst, rsem, **to):
        c = remote(src, dst, s_send.at[len(sends)], rsem, **to)
        c.start()
        sends.append(c)

    def recv(dst, rsem):
        remote(dst, dst, s_send.at[0], rsem).wait_recv()

    def image(i, j):
        return xa.at[pl.ds(mo(((i * PARTS + j) * 15 + 1) * WIDE, WIDE), ROWS)]

    def img_rows(i, j):
        return pl.ds(mo((i * PARTS + j) * ROWS, 32), ROWS)

    barrier = pltpu.get_barrier_semaphore()

    def greet(peers):
        for p in peers:
            pl.semaphore_signal(barrier, inc=1, device_id=dev(**p), device_id_type=MESH)
        pl.semaphore_wait(barrier, len(peers))

    @pl.when(st == 0)
    def _():
        loads = [
            pltpu.make_async_copy(act.at[i, :, :, zcols(q)], zs.at[i * PARTS + q], s_loc.at[i * PARTS + q])
            for i in range(3) for q in range(PARTS)
        ]
        for c in loads:
            c.start()
        greet([dict(tp=k2), dict(dp=zo), dict(stage=1, tp=qa), dict(stage=1, tp=qa + 1)])

        def to_z(i, j):
            for n in range(2):
                src = xa.at[pl.ds(mo(((i * PARTS + j) * 15 + 1) * WIDE, WIDE), ROWS), zcols(qa + n)]
                send(src, ga.at[0, qa + n, img_rows(i, j)], r_xs.at[i * PARTS + j, n], dp=zo)

        def y_image(i, j):
            send(image(i, j), image(i, j), r_x.at[i * PARTS + j], stage=1)

        def x_image(i):
            send(image(i, k), image(i, k), r_x.at[i * PARTS + k], tp=k2)

        for i in range(3):
            for c in loads[PARTS * i:PARTS * i + PARTS]:
                c.wait()

            def pad(h, _):
                rows = pl.ds(mo(((i * PARTS + k) * 15 + 1 + h) * WIDE, WIDE), WIDE)
                for q in range(PARTS):
                    xa[rows, q * LANES:q * LANES + LANES] = jnp.concatenate([zs[i * PARTS + q, h], jnp.zeros((2, LANES), BF)], axis=0)
                return 0

            lax.fori_loop(0, SIDE, pad, 0)
            if i == 0:
                x_image(0)
                y_image(0, k)
            if i == 1:
                y_image(1, k)
        x_image(2)
        x_image(1)
        for i in range(3):
            to_z(i, k)
        recv(image(0, k2), r_x.at[k2])
        y_image(0, k2)
        y_image(2, k)
        recv(image(2, k2), r_x.at[8 + k2])
        y_image(2, k2)
        recv(image(1, k2), r_x.at[PARTS + k2])
        for i in range(3):
            to_z(i, k2)
        for i in range(3):
            for j in (k, k2):
                for n in range(2):
                    buf = ga.at[0, qa + n, img_rows(i, j)]
                    recv(buf, r_xs.at[i * PARTS + j, n])
                    send(buf, xz.at[img_rows(i, j)], r_xz.at[i, j], stage=1, tp=qa + n)
        zs[...] = jnp.zeros((IMAGES, SIDE, SIDE, LANES), BF)
        fill = pltpu.make_async_copy(zs, z_out, s_loc.at[0])
        fill.start()
        fill.wait()
        for i in range(3):
            for n in range(2):
                q = qa + n
                recv(dxs.at[i * PARTS + q], r_rel.at[i, q])
                send(dxs.at[i * PARTS + q], dx_out.at[i, :, :, zcols(q)], r_dx.at[i, q], tp=k2)
        for i in range(3):
            for q in range(PARTS):
                recv(dx_out.at[i, :, :, zcols(q)], r_dx.at[i, q])
        for c in sends:
            c.wait_send()

    sends.clear()

    @pl.when(st == 1)
    def _():
        local = [
            pltpu.make_async_copy(dz_in, zs, s_loc.at[0]),
            pltpu.make_async_copy(gam_in, gamv.at[k], s_loc.at[1]),
            pltpu.make_async_copy(gs_in, gsv.at[k], s_loc.at[2]),
            pltpu.make_async_copy(wc.at[:, :, pl.ds(kc, LANES)], wr.at[pl.ds(0, TAPS), pl.ds(kc, LANES)], s_loc.at[3]),
            pltpu.make_async_copy(ws.at[:, pl.ds(kc, LANES)], wr.at[TAPS, pl.ds(kc, LANES)], s_loc.at[PARTS]),
            pltpu.make_async_copy(wc, wo.at[pl.ds(0, TAPS)], s_loc.at[5]),
            pltpu.make_async_copy(ws, wo.at[TAPS], s_loc.at[6]),
        ]
        for c in local:
            c.start()

        def zero_rows(n, _):
            xa[pl.ds(mo(n * HALO, WIDE), WIDE)] = jnp.zeros((WIDE, CHANNELS), BF)
            return 0

        lax.fori_loop(0, 13, zero_rows, 0)
        greet([dict(tp=k1), dict(tp=k2), dict(tp=k3), dict(dp=zo), dict(stage=0, tp=qa), dict(stage=0, tp=qa + 1)])

        def wdst(tap, q):
            return wr.at[tap, zcols(q)]

        mine, other = z * 5, zo * 5

        def wsend(t, q, n):
            ssem, rsem = s_send.at[len(sends)], r_wx.at[n, t]
            if t < PARTS:
                send(wc.at[mine + t, :, zcols(q)], wdst(mine + t, k), rsem, tp=q)
                return

            @pl.when(z == 0)
            def _():
                remote(wc.at[PARTS, :, zcols(q)], wdst(PARTS, k), ssem, rsem, tp=q).start()

            @pl.when(z == 1)
            def _():
                remote(ws.at[:, zcols(q)], wdst(TAPS, k), ssem, rsem, tp=q).start()

            sends.append(remote(ws.at[:, zcols(q)], wdst(TAPS, k), ssem, rsem, tp=q))

        for n, p in enumerate((k1, k2, k3)):
            send(gam_in, gamv.at[k], r_v.at[n, 0], tp=p)
            send(gs_in, gsv.at[k], r_v.at[n, 1], tp=p)
        for t in range(5):
            wsend(t, k2, 0)
            wsend(t, k3, 1)
        send(wc.at[:, :, zcols(k1)], wr.at[pl.ds(0, TAPS), pl.ds(kc, LANES)], r_ws.at[0], tp=k1)
        send(ws.at[:, zcols(k1)], wr.at[TAPS, pl.ds(kc, LANES)], r_ws.at[1], tp=k1)
        def set_up():
            for n in range(5):
                gx[pl.ds(n * HALO, WIDE)] = jnp.zeros((WIDE, CHANNELS), BF)
            for n in range(TAPS):
                gh0[pl.ds(n * HALO, WIDE)] = jnp.zeros((WIDE, LANES), BF)
                gh1[pl.ds(n * HALO, WIDE)] = jnp.zeros((WIDE, LANES), BF)
            dxs[0:3] = jnp.zeros((3, SIDE, SIDE, LANES), BF)
            for c in local:
                c.wait()
            for c in fills:
                c.start()

        fills = [
            pltpu.make_async_copy(dxs.at[pl.ds(0, 3)], dx_out.at[:, :, :, zcols(q)], s_loc.at[10 + q]) for q in range(PARTS)
        ]

        def pad_dz(n, _):
            row = (lax.rem(n, 3) * PARTS + n // 3) * ROWS
            for h in range(SIDE):
                dz[pl.ds(mo(row + h * WIDE, WIDE), WIDE)] = jnp.concatenate([zs[n, h], jnp.zeros((2, LANES), BF)], axis=0)
            return 0

        def take(i, j):
            recv(image(i, j), r_x.at[i * PARTS + j])

        def pass_on(i, j, tp):
            send(image(i, j), image(i, j), r_x.at[i * PARTS + j], tp=tp)

        def fwd(i, b, mode):
            gam, beta, gsc = gamv[k], bet[...], gsv[k]
            bases = [mo((i * PARTS + b * 2 + n) * HALO, WIDE) for n in range(2)]
            ch = {
                "all": pl.ds(0, CHANNELS),
                "own": pl.ds(mo(kx * 512, 512), 512),
                "rest": pl.ds(mo((1 - kx) * 512, 512), 512),
            }[mode]

            def lhs(t):
                return jnp.concatenate([xa[pl.ds(mo(s + t * WIDE, WIDE), ROWS), ch] for s in bases], axis=0)

            parts = []
            for j in range(3):
                acc = dot(lhs(0), wr[j, ch])
                acc += dot(lhs(1), wr[3 + j, ch])
                acc += dot(lhs(2), wr[6 + j, ch])
                parts.append(acc)
            pre = parts[1] + pltpu.roll(parts[0], 1, 0) + pltpu.roll(parts[2], 447, 0)
            u = pre * gam + dot(lhs(1), wr[TAPS, ch]) * gsc
            if mode == "own":
                for n in range(2):
                    dwa[b * 2 + n, 0:ROWS, i * LANES:i * LANES + LANES] = u[n * ROWS:n * ROWS + ROWS]
                return
            if mode == "rest":
                u += jnp.concatenate([dwa[b * 2 + n, 0:ROWS, i * LANES:i * LANES + LANES] for n in range(2)], axis=0)
            u += beta
            at = pl.ds(mo(i * SET + b * PAIR, 64), PAIR)
            zb = jnp.maximum(u, 0.0).astype(BF)
            for n in range(2):
                for h in range(SIDE):
                    zs[(b * 2 + n) * 3 + i, h] = zb[(n * SIDE + h) * WIDE:(n * SIDE + h) * WIDE + SIDE]
            ga[z, k, at] = jnp.where(u > 0.0, dz[at].astype(F32), 0.0).astype(BF)

        def fwd_set(i, mode):
            def body(b, _):
                fwd(i, b, mode)
                return 0

            lax.fori_loop(0, 2, body, 0)

        def blk(zz, q, i):
            return ga.at[zz, q, pl.ds(mo(i * SET, 128), SET)]

        def gsend(zz, q, i, **to):
            send(blk(zz, q, i), blk(zz, q, i), r_g.at[zz, q, i], **to)

        def grecv(zz, q, i):
            recv(blk(zz, q, i), r_g.at[zz, q, i])

        def put_xt(val, t):
            v = val.astype(F32)
            for j in range(3):
                w = v if j == 1 else pltpu.roll(v, (1 - j) % SET, 0)
                xt[j, :, pl.ds(t * SET, SET)] = w.T.astype(BF)

        def dx(i, n0):
            for q in range(PARTS):
                gam, gsc = gamv[q], gsv[q]

                def scale(n, _):
                    v = ga[z, q, pl.ds(mo(i * SET + n * ROWS, 32), ROWS)].astype(F32)
                    gx[pl.ds(mo(n * HALO + WIDE, WIDE), ROWS), pl.ds(q * LANES, LANES)] = (v * gam).astype(BF)
                    gsx[pl.ds(mo(n * ROWS, 32), ROWS), pl.ds(q * LANES, LANES)] = (v * gsc).astype(BF)
                    return 0

                lax.fori_loop(0, PARTS, scale, 0)

            def body(b):
                bases = [mo((b * 2 + n) * HALO, WIDE) for n in range(2)]

                def lhs(t):
                    return jnp.concatenate([gx[pl.ds(mo(s + (2 - t) * WIDE, WIDE), ROWS)] for s in bases], axis=0)

                parts = []
                for j in range(3):
                    acc = dot_t(lhs(0), wo[j])
                    acc += dot_t(lhs(1), wo[3 + j])
                    acc += dot_t(lhs(2), wo[6 + j])
                    parts.append(acc)
                tot = parts[1] + pltpu.roll(parts[0], 447, 0) + pltpu.roll(parts[2], 1, 0)
                tot += dot_t(gsx[pl.ds(mo(b * PAIR, 64), PAIR)], wo[TAPS])
                db = tot.astype(BF)
                for n in range(2):
                    for h in range(SIDE):
                        dxs[i * PARTS + b * 2 + n, h] = db[(n * SIDE + h) * WIDE:(n * SIDE + h) * WIDE + SIDE]

            def step(m, _):
                body(jnp.where(m == 0, 1 - kx, kx))

                @pl.when(m == 0)
                def _():
                    for j, via, ssem in out[0]:
                        remote(dxs.at[i * PARTS + j], dxs.at[i * PARTS + k], ssem, r_rel.at[i, k], stage=0, tp=via).start()

                @pl.when(m == 1)
                def _():
                    for j, via, ssem in out[1]:
                        remote(
                            dxs.at[i * PARTS + j], dx_out.at[i, :, :, pl.ds(kc, LANES)], ssem, r_dx.at[i, k], stage=0, tp=via
                        ).start()

                return 0

            out = (
                ((k2, k, s_send.at[n0]), (k3, k1, s_send.at[n0 + 1])),
                ((k, k, s_send.at[n0 + 2]), (k1, k1, s_send.at[n0 + 3])),
            )
            lax.fori_loop(0, 2, step, 0)

        def dx_sends(count):
            n0 = len(sends)
            for n in range(PARTS * count):
                sends.append(remote(dxs.at[0], dxs.at[0], s_send.at[n0 + n], r_rel.at[0, 0]))
            return n0

        def quarter(n):
            b = lax.rem(k + 2 * (n // 2), PARTS)
            return b + lax.rem(n, 2) * (1 - 2 * lax.rem(b, 2))

        def dw(u, first, lo, hi, between=None):
            bufs = ((gh0, gsh0), (gh1, gsh1))

            def scale(n, m):
                q = quarter(n)

                def value(r):
                    t = u * 8 + r
                    zz = z if t < IMAGES else zo
                    return ga[zz, q, pl.ds((t % IMAGES) * ROWS, ROWS)]

                scale_block(value, gamv[q], gsv[q], *bufs[m])

            def pair(half, _):
                if between is not None:
                    pl.when(half == 1)(between)
                for m in range(2):
                    n = 2 * half + m
                    cols = zcols(quarter(n))

                    def put(tap, d):
                        if first:
                            dwa[tap, :, cols] = d
                        else:
                            dwa[tap, :, cols] += d

                    if m == 0:
                        scale(n + 1, 1)
                    elif hi - lo > 1:
                        scale(jnp.minimum(n + 1, 3), 0)
                    weight_dots(xt, pl.ds(u * UNIT, UNIT), *bufs[m], put)
                    if not first:
                        pltpu.make_async_copy(dwa.at[:, :, cols], acc_out.at[:, :, cols], s_loc.at[10 + n]).start()
                return 0

            scale(2 * lo, 0)
            lax.fori_loop(lo, hi, pair, 0)

        def collect(i):
            take(i, k1)
            take(i, k3)

        def own_xt(i):
            put_xt(
                jnp.concatenate(
                    [xa[pl.ds(((i * PARTS + j) * 15 + 1) * WIDE, ROWS), pl.ds(kc, LANES)] for j in range(PARTS)], axis=0
                ),
                i,
            )

        def spread(i):
            gsend(z, k, i, tp=k2)
            gsend(z, k, i, dp=zo)
            gsend(z, k, i, tp=k1)
            own_xt(i)

        def relay(zz, q, i, ssem):
            grecv(zz, q, i)
            if ssem is None:
                gsend(zz, q, i, tp=k1)
            else:
                remote(blk(zz, q, i), blk(zz, q, i), ssem, r_g.at[zz, q, i], tp=k1).start()

        def relay_x(i, ssem=None):
            relay(z, k2, i, ssem)

        def relay_z(i, ssem=None):
            relay(zo, k, i, ssem)

        def half(zz, q, i, h):
            return ga.at[zz, q, pl.ds(i * SET + h * PAIR, PAIR)]

        def diagonal(i):
            send(half(zo, k, i, 0), half(zo, k, i, 0), r_h.at[i, 0], tp=k2)
            send(half(z, k2, i, 1), half(z, k2, i, 1), r_h.at[i, 1], dp=zo)

        def arrive(i, ssem):
            recv(half(zo, k2, i, 0), r_h.at[i, 0])
            recv(half(zo, k2, i, 1), r_h.at[i, 1])
            remote(blk(zo, k2, i), blk(zo, k2, i), ssem, r_g.at[zo, k2, i], tp=k1).start()
            for j in range(PARTS):
                recv(xz.at[pl.ds(i * SET + j * ROWS, ROWS)], r_xz.at[i, j])
            put_xt(xz[pl.ds(i * SET, SET)], 3 + i)

        def results(i, which):
            at = pl.ds((i - 1) * SET, SET)
            pairs = [(blk(zo, q, i), g_out.at[q, at]) for q in ((k1, k3) if which else (k, k2))]
            if which == 0:
                pairs.append((xt.at[:, :, pl.ds((3 + i) * SET, SET)], xt_out.at[:, :, at]))
            return [pltpu.make_async_copy(a, b, s_tail.at[i - 1, which, n]) for n, (a, b) in enumerate(pairs)]

        def leave(i, which):
            for c in results(i, which):
                c.start()

        for t in range(5):
            for s, q in ((0, k2), (1, k3)):
                recv(wdst(mine + t, q), r_wx.at[s, t])
                send(wdst(mine + t, q), wdst(mine + t, q), r_wz.at[s, t], dp=zo)
            if t == 0:
                set_up()
                for n, p in enumerate((k1, k2, k3)):
                    recv(gamv.at[p], r_v.at[n, 0])
                    recv(gsv.at[p], r_v.at[n, 1])
                recv(wr.at[pl.ds(0, TAPS), zcols(k1)], r_ws.at[0])
                recv(wr.at[TAPS, zcols(k1)], r_ws.at[1])
            if t == 1:
                lax.fori_loop(0, IMAGES, pad_dz, 0)
                take(0, k)
                pass_on(0, k, k1)
            if t == 2:
                for c in fills:
                    c.wait()
                take(0, k1)
                fwd(0, kx, "own")
            if t == 3:
                take(1, k)
                pass_on(1, k, k2)
                pass_on(1, k, k1)
        take(1, k1)
        fwd(1, kx, "own")
        take(0, k2)
        pass_on(0, k2, k1)
        take(0, k3)
        fwd(0, 1 - kx, "own")
        for t in range(5):
            for s, q in ((0, k2), (1, k3)):
                recv(wdst(other + t, q), r_wz.at[s, t])
        fwd_set(0, "rest")
        spread(0)
        fwd(1, kx, "rest")
        take(1, k2)
        pass_on(1, k2, k1)
        take(2, k)
        pass_on(2, k, k1)
        take(1, k3)
        fwd(1, 1 - kx, "all")
        spread(1)
        grecv(z, k1, 0)
        grecv(z, k1, 1)
        dw(0, True, 0, 1)
        relay_z(0)
        relay_x(0)
        diagonal(0)
        n01 = dx_sends(2)

        def dx_of(i, n0):
            grecv(z, k3, i)
            dx(i, n0)

        take(2, k2)
        pass_on(2, k2, k1)

        def first_two(i, _):
            dx_of(i, n01 + PARTS * i)

            @pl.when(i == 0)
            def _():
                collect(2)
                relay_x(1, s_send.at[nsp + 3])
                relay_z(1, s_send.at[nsp + PARTS])
                fwd_set(2, "all")
                for n, (q, to) in enumerate(own_to):
                    remote(blk(z, k, 2), blk(z, k, 2), s_send.at[nsp + n], r_g.at[z, k, 2], **to).start()
                for n, (zz, q, h, to) in enumerate(across):
                    part = half(zz, q, 1, h)
                    remote(part, part, s_send.at[nsp + 5 + n], r_h.at[1, h], **to).start()
                own_xt(2)

            return 0

        nsp = len(sends)
        own_to = ((k2, dict(tp=k2)), (k, dict(dp=zo)), (k1, dict(tp=k1)))
        across = ((zo, k, 0, dict(tp=k2)), (z, k2, 1, dict(dp=zo)))
        for n in range(5):
            sends.append(remote(blk(z, k, 2), blk(z, k, 2), s_send.at[nsp + n], r_g.at[z, k, 2]))
        for n in range(2):
            sends.append(remote(half(z, k, 2, n), half(z, k, 2, n), s_send.at[nsp + 5 + n], r_h.at[1, n]))
        lax.fori_loop(0, 2, first_two, 0)
        zcopy = pltpu.make_async_copy(zs, z_out, s_loc.at[8])
        zcopy.start()
        dw(0, True, 1, 2)
        relay_x(2)
        relay_z(2)
        diagonal(2)
        nar = len(sends)
        for i in range(3):
            sends.append(remote(blk(zo, k2, i), blk(zo, k2, i), s_send.at[nar + i], r_g.at[zo, k2, i]))
        arrive(0, s_send.at[nar])
        grecv(z, k1, 2)
        dx_of(2, dx_sends(1))
        copies = [
            pltpu.make_async_copy(gamv, gam_out, s_loc.at[6]),
            pltpu.make_async_copy(gsv, gs_out, s_loc.at[7]),
        ]
        for c in copies:
            c.start()
        arrive(1, s_send.at[nar + 1])
        leave(1, 0)
        grecv(zo, k1, 0)
        grecv(zo, k3, 0)

        def last_set():
            arrive(2, s_send.at[nar + 2])
            leave(2, 0)
            grecv(zo, k1, 1)
            grecv(zo, k3, 1)
            leave(1, 1)

        dw(1, False, 0, 2, last_set)
        grecv(zo, k1, 2)
        grecv(zo, k3, 2)
        leave(2, 1)
        tail = [c for i in (1, 2) for which in range(2) for c in results(i, which)]
        for c in tail + copies + [zcopy]:
            c.wait()
        for n in range(PARTS):
            cols = zcols(quarter(n))
            pltpu.make_async_copy(dwa.at[:, :, cols], acc_out.at[:, :, cols], s_loc.at[10 + n]).wait()
        for c in sends:
            c.wait_send()


def last_kernel(
    z_in, dx_in, acc, xt_in, g_in, gamv, gsv,
    z_out, dx_out, dw_out, ds_out,
    xt, g, gh0, gsh0, gh1, gsh1, dwa, zb, dxb,
    sem,
):
    st = lax.axis_index("stage")
    bounce = [
        (pltpu.make_async_copy(z_in, zb, sem.at[0]), pltpu.make_async_copy(zb, z_out, sem.at[1])),
        (pltpu.make_async_copy(dx_in, dxb, sem.at[2]), pltpu.make_async_copy(dxb, dx_out, sem.at[3])),
    ]

    def outs(q):
        cols = zcols(q)
        return (
            pltpu.make_async_copy(dwa.at[q, pl.ds(0, TAPS)], dw_out.at[:, :, cols], sem.at[PARTS + 2 * q]),
            pltpu.make_async_copy(dwa.at[q, TAPS], ds_out.at[:, cols], sem.at[5 + 2 * q]),
        )

    @pl.when(st == 0)
    def _():
        for c, _n in bounce:
            c.start()

        def zero(tap, _):
            for q in range(PARTS):
                dwa[q, tap] = jnp.zeros((LANES, LANES), F32)
            return 0

        lax.fori_loop(0, 10, zero, 0)
        for q in range(PARTS):
            for c in outs(q):
                c.start()
        for c, n in bounce:
            c.wait()
            n.start()
        for _c, n in bounce:
            n.wait()
        for q in range(PARTS):
            for c in outs(q):
                c.wait()

    @pl.when(st == 1)
    def _():
        loads = [pltpu.make_async_copy(g_in.at[0], g.at[0], sem.at[IMAGES])]
        loads += [pltpu.make_async_copy(xt_in.at[j], xt.at[j], sem.at[WIDE + j]) for j in range(3)]
        accs = [pltpu.make_async_copy(acc.at[:, :, zcols(q)], dwa.at[q], sem.at[20 + q]) for q in range(PARTS)]
        more = [pltpu.make_async_copy(g_in.at[q], g.at[q], sem.at[IMAGES + q]) for q in range(1, PARTS)]
        for c in [*loads, accs[0], more[0], accs[1], *more[1:], *accs[2:]]:
            c.start()
        for c, _n in bounce:
            c.start()
        for n in range(TAPS):
            gh0[pl.ds(n * HALO, WIDE)] = jnp.zeros((WIDE, LANES), BF)
            gh1[pl.ds(n * HALO, WIDE)] = jnp.zeros((WIDE, LANES), BF)
        bufs = ((gh0, gsh0), (gh1, gsh1))

        def scale(q, m):
            def value(n):
                return g[q, pl.ds(n * ROWS, ROWS)]

            scale_block(value, gamv[q], gsv[q], *bufs[m])

        loads[0].wait()
        scale(0, 0)
        for c in loads[1:]:
            c.wait()

        def pair(half, _):
            @pl.when(half == 1)
            def _():
                for c, n in bounce:
                    c.wait()
                    n.start()

            for m in range(2):
                q = 2 * half + m
                pltpu.make_async_copy(acc.at[:, :, zcols(q)], dwa.at[q], sem.at[20 + q]).wait()
                after = jnp.minimum(q + 1, 3)

                @pl.when(q < 3)
                def _():
                    pltpu.make_async_copy(g_in.at[after], g.at[after], sem.at[IMAGES + after]).wait()

                scale(after, 1 - m)

                def put(tap, d):
                    dwa[q, tap] += d

                weight_dots(xt, pl.ds(0, UNIT), *bufs[m], put)
                for c in outs(q):
                    c.start()
            return 0

        lax.fori_loop(0, 2, pair, 0)
        for _c, n in bounce:
            n.wait()
        for q in range(PARTS):
            for c in outs(q):
                c.wait()


def solution(mesh):
    act_spec = P("stage", ("dp", "tp"), None, None, None)
    kernel_spec = P("stage", None, None, "tp", None)
    short_spec = P("stage", "tp", None)
    vec_spec = P("stage", "tp")
    grad_spec = P("stage", "dp", None, None, "tp")

    def device_step(act_in, w_conv, w_short, gamma, beta, gamma_s, grad_z):
        any_spec = pl.BlockSpec(memory_space=pl.ANY)
        vm_spec = pl.BlockSpec(memory_space=pltpu.VMEM)
        dma = pltpu.SemaphoreType.DMA
        sds = jax.ShapeDtypeStruct
        z_shape, dx_shape = sds((IMAGES, SIDE, SIDE, LANES), BF), sds((3, SIDE, SIDE, CHANNELS), BF)
        block = [pltpu.VMEM((8 * HALO + WIDE, LANES), BF), pltpu.VMEM((UNIT, LANES), BF)]
        mids = pl.pallas_call(
            block_kernel,
            out_shape=(
                z_shape,
                dx_shape,
                sds((10, LANES, CHANNELS), F32),
                sds((3, LANES, UNIT), BF),
                sds((PARTS, UNIT, LANES), BF),
                sds((PARTS, 1, LANES), F32),
                sds((PARTS, 1, LANES), F32),
            ),
            in_specs=[any_spec] * 5 + [vm_spec, any_spec],
            out_specs=(any_spec,) * 7,
            scratch_shapes=[
                pltpu.VMEM((IMAGES * HALO + WIDE, CHANNELS), BF),
                pltpu.VMEM((10, LANES, CHANNELS), BF),
                pltpu.VMEM((10, CHANNELS, LANES), BF),
                pltpu.VMEM((PARTS, 1, LANES), F32),
                pltpu.VMEM((PARTS, 1, LANES), F32),
                pltpu.VMEM((IMAGES * ROWS, LANES), BF),
                pltpu.VMEM((2, PARTS, IMAGES * ROWS, LANES), BF),
                pltpu.VMEM((IMAGES * ROWS, LANES), BF),
                pltpu.VMEM((3, LANES, 24 * ROWS), BF),
                *block,
                *block,
                pltpu.VMEM((PARTS * HALO + WIDE, CHANNELS), BF),
                pltpu.VMEM((PARTS * ROWS, CHANNELS), BF),
                pltpu.VMEM((10, LANES, CHANNELS), F32),
                pltpu.VMEM((IMAGES, SIDE, SIDE, LANES), BF),
                pltpu.VMEM((IMAGES, SIDE, SIDE, LANES), BF),
                dma((100,)),
                dma((20,)),
                dma((2, 2, 3)),
                dma((2,)),
                dma((2, 5)),
                dma((2, 5)),
                dma((3, 2)),
                dma((IMAGES,)),
                dma((IMAGES, 2)),
                dma((3, PARTS)),
                dma((2, PARTS, 3)),
                dma((3, PARTS)),
                dma((3, PARTS)),
                dma((3, 2)),
            ],
            compiler_params=pltpu.CompilerParams(has_side_effects=True, collective_id=0, vmem_limit_bytes=67043328),
        )(act_in[0], w_conv[0].reshape(TAPS, LANES, CHANNELS), w_short[0], gamma, gamma_s, beta, grad_z[0])
        z, dx, dw, ds = pl.pallas_call(
            last_kernel,
            out_shape=(z_shape, dx_shape, sds((TAPS, LANES, CHANNELS), F32), sds((LANES, CHANNELS), F32)),
            in_specs=[any_spec] * 5 + [vm_spec] * 2,
            out_specs=(any_spec,) * PARTS,
            scratch_shapes=[
                pltpu.VMEM((3, LANES, UNIT), BF),
                pltpu.VMEM((PARTS, UNIT, LANES), BF),
                *block,
                *block,
                pltpu.VMEM((PARTS, 10, LANES, LANES), F32),
                pltpu.VMEM((IMAGES, SIDE, SIDE, LANES), BF),
                pltpu.VMEM((3, SIDE, SIDE, CHANNELS), BF),
                dma((24,)),
            ],
            compiler_params=pltpu.CompilerParams(vmem_limit_bytes=67043328),
        )(*mids)
        return z[None], dx[None], dw.reshape(1, 3, 3, LANES, CHANNELS), ds[None]

    return jax.shard_map(device_step, mesh=mesh, in_specs=(act_spec, kernel_spec, short_spec, vec_spec, vec_spec, vec_spec, grad_spec), out_specs=(grad_spec, act_spec, kernel_spec, short_spec), check_vma=False)
```

time: 721 us -> 123 us (0.17); the launches traced: 710 us -> 122 us
  waiting for transfers between devices: 494 us -> 0 us
  Pallas kernels: 0 us -> 121 us
  local copies, waits for them, and re-layouts: 87.7 us -> 0 us
  matrix products: 76.8 us -> 0 us
  blocking collectives: 18.8 us -> 0 us
  between operations: 14.3 us -> 0.86 us
  starting transfers between devices: 9.8 us -> 0 us
  other arithmetic: 8.7 us -> 0 us
    reduce_scatter x2 -> x0, waiting for transfers between devices: 172 us -> none  [device_step(): lax.psum_scatter((pre_part, short_part), 'tp', scatter_dimension=3, tiled...]
    psum x1 -> x0, waiting for transfers between devices: 158 us -> none  [device_step(): dw_sum, dws_sum = lax.psum((dw_part, dws_part), 'dp')]
    pallas_call x0 -> x2, Pallas kernels: none -> 121 us  [the longest x1 105 us: device_step(): pl.pallas_call(block_kernel, out_shape=(z_shape, dx_shape, sds((10, LANES...]
    all_gather x2 -> x0, waiting for transfers between devices: 88.3 us -> none  [device_step(): lax.all_gather((g_main, g_short), 'tp', axis=3, tiled=True)]
    unnamed x17 -> x0, local copies, waits for them, and re-layouts: 69.7 us -> none
    ppermute x2 -> x0, waiting for transfers between devices: 59.9 us -> none  [the longest x1 31.8 us: device_step(): act_local = lax.ppermute(by_channel, 'stage', perm=[(0, 1)])]
    conv_general_dilated x3 -> x0, matrix products: 59.7 us -> none  [the longest x2 39.2 us: conv_same(): lax.conv_general_dilated(left_op, right_op, (1, 1), 'SAME', dimension_num...]
    all_to_all x1 -> x0, blocking collectives: 18.8 us -> none  [device_step(): by_channel = lax.all_to_all(act_in[0], 'tp', 3, 0, tiled=True)]
  transfers between devices with their start and end apart: 8 -> 0, of which waited for: 8 -> 0; matrix products, arithmetic and copies ran while one was open for 8% -> 0% of each run, Pallas kernels for 0% -> 0%
where the time goes in v3:
time: 123 us; the launch traced here: 122 us
  Pallas kernels  121 us (98%)
    pallas_call x1, Pallas kernels, device_step(): pl.pallas_call(block_kernel, out_shape=(z_shape, dx_shape, sds((10, LANES...  105 us
    pallas_call x1, Pallas kernels, device_step(): pl.pallas_call(last_kernel, out_shape=(z_shape, dx_shape, sds((TAPS, LANE...  16.2 us

profile of v3, /device:TPU:5, one launch (start us, length us, event | category | flops | bytes accessed | tf_op | source)
XLA Modules:
  0.0 122.3 jit_solution(18100380002038639869)
XLA Ops:
  0.6 105.3 %shard_map.102 = (bf16[12,14,14,256]{3,2,1,0:T(8,128)(2,1)}, bf16[3,14,14,1024]{3,2,1,0:T(8,128)(2,1)}, f32[10,256,1024]{2,1,0:T(8,128)}, bf16[3,256,1792]{2,1,0...) custom-call(bf16[3,14,14,1024]{3,2,1,0:T(8,128)(2,1)} %bitcast.9, ...), custom_call_target="tpu_custom_call" | custom-call | tf_op jit(solution)/shard_map/pallas_call | solution.py:712
  105.9 16.2 %shard_map.103 = (bf16[12,14,14,256]{3,2,1,0:T(8,128)(2,1)}, bf16[3,14,14,1024]{3,2,1,0:T(8,128)(2,1)}, f32[9,256,1024]{2,1,0:T(8,128)}, f32[256,1024]{1,0:T(8,128)}) custom-call(bf16[12,14,14,256]{3,2,1,0:T(8,128)(2,1)} %get-tuple-element.15.z_in, bf16[3,14,14,1024]{3,2,1,0:T(8,128)(2,1)} %get-tuple-element.16.dx_in, ...), custom_call_target="tpu_custom_call" | custom-call | tf_op jit(solution)/shard_map/pallas_call | solution.py:759

commit v4 on v3

--- a/solution.py
+++ b/solution.py
@@ -370,7 +370,7 @@
             b = lax.rem(k + 2 * (n // 2), PARTS)
             return b + lax.rem(n, 2) * (1 - 2 * lax.rem(b, 2))
 
-        def dw(u, first, lo, hi, between=None):
+        def dw(u, first, lo, hi):
             bufs = ((gh0, gsh0), (gh1, gsh1))
 
             def scale(n, m):
@@ -384,8 +384,6 @@
                 scale_block(value, gamv[q], gsv[q], *bufs[m])
 
             def pair(half, _):
-                if between is not None:
-                    pl.when(half == 1)(between)
                 for m in range(2):
                     n = 2 * half + m
                     cols = zcols(quarter(n))
@@ -412,7 +410,10 @@
             take(i, k1)
             take(i, k3)
 
-        def own_xt(i):
+        def spread(i):
+            gsend(z, k, i, tp=k2)
+            gsend(z, k, i, dp=zo)
+            gsend(z, k, i, tp=k1)
             put_xt(
                 jnp.concatenate(
                     [xa[pl.ds(((i * PARTS + j) * 15 + 1) * WIDE, ROWS), pl.ds(kc, LANES)] for j in range(PARTS)], axis=0
@@ -420,50 +421,33 @@
                 i,
             )
 
-        def spread(i):
-            gsend(z, k, i, tp=k2)
-            gsend(z, k, i, dp=zo)
-            gsend(z, k, i, tp=k1)
-            own_xt(i)
-
-        def relay(zz, q, i, ssem):
-            grecv(zz, q, i)
-            if ssem is None:
-                gsend(zz, q, i, tp=k1)
+        def relay_x(i):
+            grecv(z, k2, i)
+            gsend(z, k2, i, tp=k1)
+
+        def relay_z(i):
+            grecv(zo, k, i)
+            gsend(zo, k, i, tp=k1)
+
+        def half(zz, q, h):
+            return ga.at[zz, q, pl.ds(2 * SET + h * PAIR, PAIR)]
+
+        def diagonal(i):
+            if i == 0:
+                gsend(zo, k, 0, tp=k2)
+            if i == 1:
+                gsend(z, k2, 1, dp=zo)
+            if i == 2:
+                send(half(zo, k, 0), half(zo, k, 0), r_h.at[0], tp=k2)
+                send(half(z, k2, 1), half(z, k2, 1), r_h.at[1], dp=zo)
+
+        def diagonal_recv(i):
+            if i == 2:
+                recv(half(zo, k2, 0), r_h.at[0])
+                recv(half(zo, k2, 1), r_h.at[1])
             else:
-                remote(blk(zz, q, i), blk(zz, q, i), ssem, r_g.at[zz, q, i], tp=k1).start()
-
-        def relay_x(i, ssem=None):
-            relay(z, k2, i, ssem)
-
-        def relay_z(i, ssem=None):
-            relay(zo, k, i, ssem)
-
-        def half(zz, q, i, h):
-            return ga.at[zz, q, pl.ds(i * SET + h * PAIR, PAIR)]
-
-        def diagonal(i):
-            send(half(zo, k, i, 0), half(zo, k, i, 0), r_h.at[i, 0], tp=k2)
-            send(half(z, k2, i, 1), half(z, k2, i, 1), r_h.at[i, 1], dp=zo)
-
-        def arrive(i, ssem):
-            recv(half(zo, k2, i, 0), r_h.at[i, 0])
-            recv(half(zo, k2, i, 1), r_h.at[i, 1])
-            remote(blk(zo, k2, i), blk(zo, k2, i), ssem, r_g.at[zo, k2, i], tp=k1).start()
-            for j in range(PARTS):
-                recv(xz.at[pl.ds(i * SET + j * ROWS, ROWS)], r_xz.at[i, j])
-            put_xt(xz[pl.ds(i * SET, SET)], 3 + i)
-
-        def results(i, which):
-            at = pl.ds((i - 1) * SET, SET)
-            pairs = [(blk(zo, q, i), g_out.at[q, at]) for q in ((k1, k3) if which else (k, k2))]
-            if which == 0:
-                pairs.append((xt.at[:, :, pl.ds((3 + i) * SET, SET)], xt_out.at[:, :, at]))
-            return [pltpu.make_async_copy(a, b, s_tail.at[i - 1, which, n]) for n, (a, b) in enumerate(pairs)]
-
-        def leave(i, which):
-            for c in results(i, which):
-                c.start()
+                grecv(zo, k2, i)
+            gsend(zo, k2, i, tp=k1)
 
         for t in range(5):
             for s, q in ((0, k2), (1, k3)):
@@ -513,77 +497,71 @@
         dw(0, True, 0, 1)
         relay_z(0)
         relay_x(0)
-        diagonal(0)
-        n01 = dx_sends(2)
-
-        def dx_of(i, n0):
-            grecv(z, k3, i)
-            dx(i, n0)
-
         take(2, k2)
         pass_on(2, k2, k1)
-
-        def first_two(i, _):
-            dx_of(i, n01 + PARTS * i)
-
-            @pl.when(i == 0)
-            def _():
-                collect(2)
-                relay_x(1, s_send.at[nsp + 3])
-                relay_z(1, s_send.at[nsp + PARTS])
-                fwd_set(2, "all")
-                for n, (q, to) in enumerate(own_to):
-                    remote(blk(z, k, 2), blk(z, k, 2), s_send.at[nsp + n], r_g.at[z, k, 2], **to).start()
-                for n, (zz, q, h, to) in enumerate(across):
-                    part = half(zz, q, 1, h)
-                    remote(part, part, s_send.at[nsp + 5 + n], r_h.at[1, h], **to).start()
-                own_xt(2)
-
-            return 0
-
-        nsp = len(sends)
-        own_to = ((k2, dict(tp=k2)), (k, dict(dp=zo)), (k1, dict(tp=k1)))
-        across = ((zo, k, 0, dict(tp=k2)), (z, k2, 1, dict(dp=zo)))
-        for n in range(5):
-            sends.append(remote(blk(z, k, 2), blk(z, k, 2), s_send.at[nsp + n], r_g.at[z, k, 2]))
-        for n in range(2):
-            sends.append(remote(half(z, k, 2, n), half(z, k, 2, n), s_send.at[nsp + 5 + n], r_h.at[1, n]))
-        lax.fori_loop(0, 2, first_two, 0)
+        collect(2)
+        fwd_set(2, "all")
+        spread(2)
         zcopy = pltpu.make_async_copy(zs, z_out, s_loc.at[8])
         zcopy.start()
-        dw(0, True, 1, 2)
+        diagonal(0)
+        relay_x(1)
+        diagonal(1)
+        relay_z(1)
+        n01 = dx_sends(2)
+
+        def dx01(i, _):
+            grecv(z, k3, i)
+            dx(i, n01 + PARTS * i)
+            return 0
+
+        lax.fori_loop(0, 2, dx01, 0)
         relay_x(2)
         relay_z(2)
         diagonal(2)
-        nar = len(sends)
-        for i in range(3):
-            sends.append(remote(blk(zo, k2, i), blk(zo, k2, i), s_send.at[nar + i], r_g.at[zo, k2, i]))
-        arrive(0, s_send.at[nar])
+        dw(0, True, 1, 2)
         grecv(z, k1, 2)
-        dx_of(2, dx_sends(1))
+        grecv(z, k3, 2)
+        dx(2, dx_sends(1))
         copies = [
             pltpu.make_async_copy(gamv, gam_out, s_loc.at[6]),
             pltpu.make_async_copy(gsv, gs_out, s_loc.at[7]),
         ]
         for c in copies:
             c.start()
-        arrive(1, s_send.at[nar + 1])
-        leave(1, 0)
+        tail = []
+
+        def leave(src, dst):
+            c = pltpu.make_async_copy(src, dst, s_tail.at[len(tail)])
+            c.start()
+            tail.append(c)
+
+        def arrive(i):
+            diagonal_recv(i)
+            for j in range(PARTS):
+                recv(xz.at[pl.ds(i * SET + j * ROWS, ROWS)], r_xz.at[i, j])
+            put_xt(xz[pl.ds(i * SET, SET)], 3 + i)
+
+        def leave_early(i):
+            at = pl.ds((i - 1) * SET, SET)
+            leave(xt.at[:, :, pl.ds((3 + i) * SET, SET)], xt_out.at[:, :, at])
+            for q in (k, k2):
+                leave(blk(zo, q, i), g_out.at[q, at])
+
+        arrive(0)
+        arrive(1)
+        leave_early(1)
         grecv(zo, k1, 0)
         grecv(zo, k3, 0)
-
-        def last_set():
-            arrive(2, s_send.at[nar + 2])
-            leave(2, 0)
-            grecv(zo, k1, 1)
-            grecv(zo, k3, 1)
-            leave(1, 1)
-
-        dw(1, False, 0, 2, last_set)
-        grecv(zo, k1, 2)
-        grecv(zo, k3, 2)
-        leave(2, 1)
-        tail = [c for i in (1, 2) for which in range(2) for c in results(i, which)]
+        dw(1, False, 0, 2)
+        arrive(2)
+        leave_early(2)
+        for i in (1, 2):
+            at = pl.ds((i - 1) * SET, SET)
+            grecv(zo, k1, i)
+            grecv(zo, k3, i)
+            for q in (k1, k3):
+                leave(blk(zo, q, i), g_out.at[q, at])
         for c in tail + copies + [zcopy]:
             c.wait()
         for n in range(PARTS):
@@ -741,7 +719,7 @@
                 pltpu.VMEM((IMAGES, SIDE, SIDE, LANES), BF),
                 dma((100,)),
                 dma((20,)),
-                dma((2, 2, 3)),
+                dma((10,)),
                 dma((2,)),
                 dma((2, 5)),
                 dma((2, 5)),
@@ -752,7 +730,7 @@
                 dma((2, PARTS, 3)),
                 dma((3, PARTS)),
                 dma((3, PARTS)),
-                dma((3, 2)),
+                dma((2,)),
             ],
             compiler_params=pltpu.CompilerParams(has_side_effects=True, collective_id=0, vmem_limit_bytes=67043328),
         )(act_in[0], w_conv[0].reshape(TAPS, LANES, CHANNELS), w_short[0], gamma, gamma_s, beta, grad_z[0])

time: 123 us -> 121 us (0.984)
  no operation moved by 1% of the time
where the time goes in v4:
time: 121 us
  Pallas kernels  120 us (99%)
    pallas_call x1, Pallas kernels, device_step(): pl.pallas_call(block_kernel, out_shape=(z_shape, dx_shape, sds((10, LANES...  104 us
    pallas_call x1, Pallas kernels, device_step(): pl.pallas_call(last_kernel, out_shape=(z_shape, dx_shape, sds((TAPS, LANE...  16.2 us

profile of v4, /device:TPU:5, one launch (start us, length us, event | category | flops | bytes accessed | tf_op | source)
XLA Modules:
  0.0 121.1 jit_solution(8909559532833699021)
XLA Ops:
  0.6 104.1 %shard_map.102 = (bf16[12,14,14,256]{3,2,1,0:T(8,128)(2,1)}, bf16[3,14,14,1024]{3,2,1,0:T(8,128)(2,1)}, f32[10,256,1024]{2,1,0:T(8,128)}, bf16[3,256,1792]{2,1,0...) custom-call(bf16[3,14,14,1024]{3,2,1,0:T(8,128)(2,1)} %bitcast.9, ...), custom_call_target="tpu_custom_call" | custom-call | tf_op jit(solution)/shard_map/pallas_call | solution.py:690
  104.7 16.2 %shard_map.103 = (bf16[12,14,14,256]{3,2,1,0:T(8,128)(2,1)}, bf16[3,14,14,1024]{3,2,1,0:T(8,128)(2,1)}, f32[9,256,1024]{2,1,0:T(8,128)}, f32[256,1024]{1,0:T(8,128)}) custom-call(bf16[12,14,14,256]{3,2,1,0:T(8,128)(2,1)} %get-tuple-element.15.z_in, bf16[3,14,14,1024]{3,2,1,0:T(8,128)(2,1)} %get-tuple-element.16.dx_in, ...), custom_call_target="tpu_custom_call" | custom-call | tf_op jit(solution)/shard_map/pallas_call | solution.py:737
